TPU v7x, 32 devices: a whole 2x2x4 slice. The times are simulated.
32 devices in a mesh: dp: 8 (over z, x), tensor: 4 (over y, core).
Axes of the slice: x: 2, y: 2, z: 4, core: 2. Of those that a mesh axis runs over, the one named last changes fastest.
Arguments:
- inputs: bfloat16 [8, 1024, 512], P('dp', 'tensor'), may hold values from -18 to 18, as said below
- lengths: int32 [8], P('dp'), may hold values from 256 to 1024
- cotangent: bfloat16 [8, 1024, 512], P('dp', 'tensor'), may hold values from -6 to 6
- ln_gains: float32 [2, 2, 512], replicated, may hold values from 0.5 to 1.5
- ln_biases: float32 [2, 2, 512], replicated, may hold values from -0.5 to 0.5
- w_query: bfloat16 [2, 512, 512], P(None, None, 'tensor'), may hold values from -0.25 to 0.25
- w_key: bfloat16 [2, 512, 512], P(None, None, 'tensor'), may hold values from -0.25 to 0.25
- w_value: bfloat16 [2, 512, 512], P(None, None, 'tensor'), may hold values from -0.25 to 0.25
- w_output: bfloat16 [2, 512, 512], P(None, 'tensor'), may hold values from -1.5 to 1.5
- w_in: bfloat16 [2, 512, 2048], P(None, None, 'tensor'), may hold values from -0.25 to 0.25
- b_in: bfloat16 [2, 2048], P(None, 'tensor'), may hold values from -1.5 to 1.5
- w_out: bfloat16 [2, 2048, 512], P(None, 'tensor'), may hold values from -0.125 to 0.125
- b_out: float32 [2, 512], replicated, may hold values from -1.5 to 1.5
Outputs:
- outputs: float32 [8, 1024, 512], P('dp', 'tensor')
- input_grad: float32 [8, 1024, 512], P('dp', 'tensor')
- grad_ln_gains: float32 [2, 2, 512], replicated
- grad_ln_biases: float32 [2, 2, 512], replicated
- grad_w_query: float32 [2, 512, 512], P(None, None, 'tensor')
- grad_w_key: float32 [2, 512, 512], P(None, None, 'tensor')
- grad_w_value: float32 [2, 512, 512], P(None, None, 'tensor')
- grad_w_output: float32 [2, 512, 512], P(None, 'tensor')
- grad_w_in: float32 [2, 512, 2048], P(None, None, 'tensor')
- grad_b_in: float32 [2, 2048], P(None, 'tensor')
- grad_w_out: float32 [2, 2048, 512], P(None, 'tensor')
- grad_b_out: float32 [2, 512], replicated
- norms: float32 [6], replicated
Inputs may be any that keep to these rules, and one draw needn't show every extreme that they name: The first lengths[s] positions of sequence s are valid, the rest padding. `inputs`: the block's input.
All inputs are finite; a program needn't handle non-finite values.
Results may differ from a plain program's by a relative error of at most 0.023.
Values may be sent and summed in bfloat16 or wider, within the bound.
No kernel may reach another device: no remote copies, remote signals or barrier semaphores. Data moves between devices by JAX's collectives and lax.ppermute only.
A program may use at most 192 MiB of HBM per device.

v0:
```python
import functools
import math

import jax
import jax.numpy as jnp
import numpy as np
from jax import lax
from jax.experimental import pallas as pl
from jax.experimental.pallas import tpu as pltpu
from jax.sharding import PartitionSpec as P

F32 = jnp.float32
BF16 = jnp.bfloat16

LAYERS = 2
ROWS = 256
WIDTH = 512
PIECES = 8
SLOTS = 4
HEAD_PAIR = 128
TILE = 64
CTX = 672
NEG = -1e30

FIRST = (0, 256, 384, 448, 480)
LAST = (240, 368, 432, 464, 480)
LEVEL_SIZE = (256, 128, 64, 32, 16)
CTX_PREV = (0, 288, 448, 544, 608)
CTX_OWN = (16, 304, 464, 560, None)
CTX_NEXT = (272, 432, 528, 592, 624)
CTX_Y = 640
CTX_DIAG = 656
TILES = (
    (0, 0, 96, 0),
    (64, 64, 96, 0),
    (128, 128, 96, 0),
    (192, 192, 96, 0),
    (256, 288, 96, 1),
    (320, 352, 96, 1),
    (384, 448, 96, 1),
    (448, 544, 128, 2),
)


def dot(left, right):
    return lax.dot_general(left, right, (((1,), (0,)), ((), ())), preferred_element_type=F32)


def dot_nt(left, right):
    return lax.dot_general(left, right, (((1,), (1,)), ((), ())), preferred_element_type=F32)


def dot_tn(left, right):
    return lax.dot_general(left, right, (((0,), (0,)), ((), ())), preferred_element_type=F32)


def iota(dims, axis):
    return lax.broadcasted_iota(jnp.int32, dims, axis)


def by_level(index, values, rest):
    result = jnp.full(index.shape, rest, jnp.int32)
    for edge, value in reversed(tuple(zip((128, 192, 224, 240, 248), values))):
        result = jnp.where(index < edge, value, result)
    return result


def spread_table(transposed=False):
    shape = (ROWS, ROWS)
    position, coarse = iota(shape, 0), iota(shape, 1)
    if transposed:
        position, coarse = coarse, position
    level = by_level(coarse, (1, 2, 3, 4, 5), 0)
    base = by_level(coarse, (0, 128, 192, 224, 240), -ROWS)
    match = jnp.right_shift(position, level) == coarse - base
    return jnp.where(match, 1.0, 0.0).astype(BF16)


def step_inverse():
    index = iota((ROWS, HEAD_PAIR), 0)
    return 1.0 / by_level(index, (2, 4, 8, 16, 32), 1).astype(F32)


def fill_bias(bias_ref):
    query = iota((2 * TILE, 128), 0) & (TILE - 1)
    key = iota((2 * TILE, 128), 1)
    block = (key >> 4) - (query >> 4)
    near = (block >= 0) & (block <= 2) & (key < 96)
    far = jnp.abs(((query + 16) >> 3) - (key >> 3)) >= 2
    coarse = near & far
    bias_ref[0] = jnp.where(near, 0.0, NEG)
    bias_ref[1] = jnp.where(coarse, 0.0, NEG)
    half = ((query & 15) >> 3) + 2
    other = jnp.where(key < 80, (key >> 3) - 8, (key >> 3) - 6)
    fourth = (query >= 32) & (query < 48) & (key >= 64) & (key < 96) & (jnp.abs(half - other) >= 2)
    third = (query < 32) & (key < 64) & coarse
    fifth = (query >= 48) & (query < 56) & (key >= 96) & ((key & 15) < 8)
    bias_ref[2] = jnp.where(third | fourth | fifth, 0.0, NEG)


def fill_count(info_ref, count_ref):
    rest, close, rank = info_ref[0], info_ref[2], info_ref[4]

    def put(row, first, size, level, owner=0, usable=1):
        place = (iota((size, HEAD_PAIR), 0) + first) * 2**level + owner * ROWS
        inside = (place + rank * ROWS >= 0) & (usable == 1)
        held = jnp.where(inside, jnp.clip(rest - place, 0, 2**level), 0)
        count_ref[row : row + size, :] = held.astype(F32).astype(BF16)

    for level in range(5):
        put(CTX_PREV[level], -16, 16, level)
        put(CTX_NEXT[level], LEVEL_SIZE[level], 16, level)
        if CTX_OWN[level] is not None:
            put(CTX_OWN[level], 0, LEVEL_SIZE[level], level)
    for row, bits, usable in ((CTX_Y, 2, 1), (CTX_DIAG, 3, 1 - close)):
        place = iota((16, HEAD_PAIR), 0) * 32 + ((rank ^ bits) - rank) * ROWS
        inside = (iota((16, HEAD_PAIR), 0) < 8) & (usable == 1)
        held = jnp.where(inside, jnp.clip(rest - place, 0, 32), 0)
        count_ref[row : row + 16, :] = held.astype(F32).astype(BF16)


def halo_table(info_ref):
    even, close = info_ref[1] == 1, info_ref[2] == 1
    position, column = iota((ROWS, 192), 0), iota((ROWS, 192), 1)
    row = jnp.where(column < 80, column, column - 80)
    level, offset = row >> 4, row & 15
    first = offset
    last = jnp.right_shift(ROWS, level) - 16 + offset
    core = jnp.where(even, last, first)
    diag = jnp.where(close, jnp.where(even, first, last), -1)
    top = jnp.where(offset < 8, offset, -1)
    diag_top = jnp.where(close, -1, top)
    index = jnp.where(
        column < 80, core, jnp.where(column < 160, diag, jnp.where(column < 176, diag_top, top))
    )
    level = jnp.where(column < 160, level, 5)
    return jnp.where(jnp.right_shift(position, level) == index, 1.0, 0.0).astype(BF16)


def halo_step():
    row = iota((192, HEAD_PAIR), 0)
    level = jnp.where(row < 160, jnp.where(row < 80, row, row - 80) >> 4, 5)
    return 1.0 / jnp.left_shift(1, level).astype(F32)


def normalize(values):
    center = values - jnp.mean(values, axis=-1, keepdims=True)
    spread = jnp.mean(center * center, axis=-1, keepdims=True)
    scale = lax.rsqrt(spread + 1e-05)
    return center * scale, scale


def by_rows(body, sums=0):
    totals = tuple(jnp.zeros((8, WIDTH), F32) for _ in range(sums))
    for start in range(0, ROWS, 32):
        totals = body(pl.ds(start, 32), totals)
    return [jnp.sum(t, axis=0, keepdims=True) for t in totals]


def fold(total, values):
    return total + jnp.sum(values.reshape(4, 8, WIDTH), axis=0)


def valid_rows(info_ref, rows):
    return iota((32, WIDTH), 0) + rows.start < info_ref[0]


def normalize_back(values, gain, grad, totals):
    hat, scale = normalize(values)
    inner = grad * gain
    mean = jnp.mean(inner, axis=-1, keepdims=True)
    along = jnp.mean(inner * hat, axis=-1, keepdims=True)
    result = scale * (inner - mean - hat * along)
    return result, (fold(totals[0], grad * hat), fold(totals[1], grad))


def gelu_parts(values):
    size = jnp.abs(values) * (1.0 / math.sqrt(2.0))
    ratio = 1.0 / (1.0 + 0.3275911 * size)
    bell = jnp.exp(-size * size)
    poly = ratio * (
        0.254829592
        + ratio * (-0.284496736 + ratio * (1.421413741 + ratio * (-1.453152027 + ratio * 1.061405429)))
    )
    tail = 0.5 * poly * bell
    share = jnp.where(values >= 0.0, 1.0 - tail, tail)
    slope = share + values * bell * (1.0 / math.sqrt(2.0 * math.pi))
    return values * share, slope


def row_mask(info_ref, shape):
    return lax.broadcasted_iota(jnp.int32, shape, 0) < info_ref[0]


def project(
    normed, weights, info_ref, spread_t, step_inv, qkv_ref, core_ref, diag_ref, far_ref, slots=SLOTS
):
    even = info_ref[1] == 1
    keep = row_mask(info_ref, (ROWS, 3 * HEAD_PAIR))
    column = lax.broadcasted_iota(jnp.int32, (ROWS, 3 * HEAD_PAIR), 1)
    column_scale = jnp.where(column < HEAD_PAIR, 0.125, 1.0)
    step_wide = jnp.concatenate([step_inv, step_inv], axis=1)
    for slot in range(slots):
        rounded = dot(normed, weights[:, slot * 384 : (slot + 1) * 384]).astype(BF16).astype(F32)
        exact = (jnp.where(keep, rounded, 0.0) * column_scale).astype(BF16)
        qkv_ref[slot, :ROWS, :] = exact
        pooled = dot(spread_t, exact)
        qkv_ref[slot, ROWS:, : 2 * HEAD_PAIR] = (pooled[:, : 2 * HEAD_PAIR] * step_wide).astype(BF16)
        qkv_ref[slot, ROWS:, 2 * HEAD_PAIR :] = pooled[:, 2 * HEAD_PAIR :].astype(BF16)
        for level in range(5):
            first = qkv_ref[slot, FIRST[level] : FIRST[level] + 16, HEAD_PAIR:]
            last = qkv_ref[slot, LAST[level] : LAST[level] + 16, HEAD_PAIR:]
            core_ref[slot, level * 16 : level * 16 + 16, :] = jnp.where(even, last, first)
            diag_ref[slot, level * 16 : level * 16 + 16, :] = jnp.where(even, first, last)
        qkv_ref.flush_part(slot)
        top = qkv_ref[slot, 496:512, HEAD_PAIR:]
        diag_ref[slot, 80:96, :] = top
        far_ref[slot, :, :] = top


def first_near_kernel(
    info_ref, x_ref, gain_ref, offset_ref, weights,
    normed_ref, stream_ref, qkv_ref, core_ref, diag_ref, far_ref,
):
    ready(x_ref, gain_ref, offset_ref)

    def start(rows, totals):
        stream = x_ref[0, rows, :].astype(F32)
        stream_ref[rows, :] = stream
        hat, _ = normalize(stream)
        normed_ref[rows, :] = (hat * gain_ref[0, 0:1, :] + offset_ref[0, 0:1, :]).astype(BF16)
        return totals

    by_rows(start)
    normed_ref.flush()
    stream_ref.flush()
    project(
        normed_ref[...], weights, info_ref, spread_table(True), step_inverse(),
        qkv_ref, core_ref, diag_ref, far_ref, 2,
    )


def first_kernel(
    info_ref, normed_ref, weights, near_core, near_diag, near_far,
    qkv_ref, core_ref, diag_ref, far_ref, part_core, part_diag, part_far,
):
    spread_t, step_inv = spread_table(True), step_inverse()
    parts = (part_core, part_diag, part_far)
    project(normed_ref[...], weights, info_ref, spread_t, step_inv, qkv_ref, *parts, 2)
    for near, part, target in zip(
        (near_core, near_diag, near_far), parts, (core_ref, diag_ref, far_ref)
    ):
        target[0:2] = near[...]
        target[2:4] = part[...]
        target.flush()


def head_stack(values):
    column = iota(values.shape, 1) & (HEAD_PAIR - 1)
    zero = jnp.zeros_like(values)
    left = jnp.where(column < HEAD_PAIR // 2, values, zero)
    right = jnp.where(column < HEAD_PAIR // 2, zero, values)
    return jnp.concatenate([left, right], axis=0)


def head_join(stacked):
    column = iota((TILE, stacked.shape[1]), 1) & (HEAD_PAIR - 1)
    return jnp.where(column < HEAD_PAIR // 2, stacked[:TILE], stacked[TILE:])


def mix_kernel(
    layer, info_ref, qkv_ref, core_ref, diag_ref, far_ref, stream_ref, gain_ref, offset_ref, weights_ref,
    ctx_ref, mixed_ref, inverse_ref, middle_ref, normed_ref, stat_ref,
    pair_ref, sum_ref, bias_ref, count_ref, spread_ref,
):
    even = info_ref[1] == 1
    near = info_ref[2] == 1
    fill_bias(bias_ref)
    fill_count(info_ref, count_ref)
    spread_ref[...] = spread_table()
    for slot in range(SLOTS):
        for level in range(5):
            rows = slice(level * 16, level * 16 + 16)
            core = core_ref[slot ^ 1, rows, :]
            diag = diag_ref[slot ^ 3, rows, :]
            diag = jnp.where(near, diag, jnp.zeros_like(diag))
            ctx_ref[slot, CTX_PREV[level] : CTX_PREV[level] + 16, :] = jnp.where(even, diag, core)
            ctx_ref[slot, CTX_NEXT[level] : CTX_NEXT[level] + 16, :] = jnp.where(even, core, diag)
            if CTX_OWN[level] is not None:
                own = slice(CTX_OWN[level], CTX_OWN[level] + LEVEL_SIZE[level])
                source = slice(FIRST[level], FIRST[level] + LEVEL_SIZE[level])
                ctx_ref[slot, own, :] = qkv_ref[slot, source, HEAD_PAIR:]
        ctx_ref[slot, CTX_Y : CTX_Y + 16, :] = far_ref[slot ^ 2, :, :]
        diag = diag_ref[slot ^ 3, 80:96, :]
        ctx_ref[slot, CTX_DIAG : CTX_DIAG + 16, :] = jnp.where(near, jnp.zeros_like(diag), diag)

    ctx_ref.flush()
    ready(qkv_ref)
    begin(weights_ref, stream_ref, gain_ref, offset_ref)

    @pl.loop(0, SLOTS)
    def _(slot):
        for query_row, context_row, keys, mask in TILES:
            queries = head_stack(qkv_ref[slot, query_row : query_row + TILE, :HEAD_PAIR])
            context = slice(context_row, context_row + keys)
            scores = dot_nt(queries, ctx_ref[slot, context, :HEAD_PAIR])
            weights = jnp.exp(scores + bias_ref[mask, :, :keys]).astype(BF16)
            values = jnp.concatenate(
                [ctx_ref[slot, context, HEAD_PAIR:], count_ref[context, :]], axis=1
            )
            pair_ref[slot, query_row : query_row + TILE, :] = head_join(dot(weights, values))

    spread = spread_ref[...]
    for slot in range(SLOTS):
        coarse = pair_ref[slot, ROWS:, :]
        high = coarse.astype(BF16)
        low = (coarse - high.astype(F32)).astype(BF16)
        total = pair_ref[slot, :ROWS, :] + dot(spread, high) + dot(spread, low)
        inverse = 1.0 / total[:, HEAD_PAIR:]
        columns = slice(slot * HEAD_PAIR, (slot + 1) * HEAD_PAIR)
        inverse_ref[:, columns] = inverse
        mixed_ref[:, columns] = (total[:, :HEAD_PAIR] * inverse).astype(BF16)
    inverse_ref.flush()
    mixed_ref.flush()
    sum_ref[...] = dot(mixed_ref[...], weights_ref[...])
    ready(stream_ref, gain_ref, offset_ref)

    def finish(rows, totals):
        attended = sum_ref[rows, :]
        squares = jnp.where(valid_rows(info_ref, rows), attended * attended, 0.0)
        middle = stream_ref[rows, :] + attended
        middle_ref[rows, :] = middle
        hat, _ = normalize(middle)
        gain, offset = gain_ref[layer, 1:2, :], offset_ref[layer, 1:2, :]
        normed_ref[rows, :] = (hat * gain + offset).astype(BF16)
        return (fold(totals[0], squares),)

    (stat_ref[...],) = by_rows(finish, 1)


def halves(half):
    start = pl.multiple_of(half * 256, 256)
    return pl.ds(start, 256), pl.ds(512 + start, 256)


def feed_slots(normed, weights, following, act_ref, slope_ref, total_ref, fresh):
    for slot, weight in enumerate(weights):
        ready(weight)
        begin(*following[slot])
        hidden = dot(normed, weight[:512, :]) + weight[1024:1025, :].astype(F32)
        act, slope = gelu_parts(hidden)
        act = act.astype(BF16)
        act_ref[slot, :, :] = act
        slope_ref[slot, :, :] = slope.astype(BF16)
        act_ref.flush_part(slot)
        slope_ref.flush_part(slot)
        part = dot(act, weight[512:1024, :])
        if slot == 0 and fresh:
            total_ref[...] = part
        else:
            total_ref[...] += part


def feed_near_kernel(info_ref, normed_ref, w0, w1, act_ref, slope_ref, total_ref):
    feed_slots(normed_ref[...], (w0, w1), ((), ()), act_ref, slope_ref, total_ref, True)


def feed_kernel(
    info_ref, normed_ref, middle_ref, w0, w1, near_ref, bias_out_ref,
    gain_ref, offset_ref, projections,
    act_ref, slope_ref, stat_ref, stream_ref, next_ref, qkv_ref, core_ref, diag_ref, far_ref,
    total_ref,
):
    following = ((near_ref, middle_ref, bias_out_ref, gain_ref, offset_ref), (projections,))
    feed_slots(normed_ref[...], (w0, w1), following, act_ref, slope_ref, total_ref, True)
    ready(near_ref)
    ready(middle_ref, bias_out_ref, gain_ref, offset_ref)

    def finish(rows, totals):
        total_ref[rows, :] += near_ref[rows, :]
        stream, totals = add_branch(info_ref, rows, totals, total_ref, bias_out_ref[0:1, :], middle_ref)
        stream_ref[rows, :] = stream
        hat, _ = normalize(stream)
        next_ref[rows, :] = (hat * gain_ref[1, 0:1, :] + offset_ref[1, 0:1, :]).astype(BF16)
        return totals

    stat_ref[0:1, :], stat_ref[1:2, :] = by_rows(finish, 2)
    stream_ref.flush()
    next_ref.flush()
    project(
        next_ref[...], projections, info_ref, spread_table(True), step_inverse(),
        qkv_ref, core_ref, diag_ref, far_ref,
    )


def add_branch(info_ref, rows, totals, branch_ref, bias, middle_ref):
    branch = branch_ref[rows, :] + bias
    stream = middle_ref[rows, :] + branch
    valid = valid_rows(info_ref, rows)
    return stream, (
        fold(totals[0], jnp.where(valid, branch * branch, 0.0)),
        fold(totals[1], jnp.where(valid, stream * stream, 0.0)),
    )


def put_grads(target, matrix, value, at=0):
    low = value.astype(BF16)
    for piece in range(PIECES):
        target[piece, matrix * 64 : matrix * 64 + 64, at : at + value.shape[1]] = low[
            piece * 64 : piece * 64 + 64
        ]


def put_half(in_target, out_target, start, half, in_grad, out_grad):
    columns, _ = halves(half)
    low = in_grad.astype(BF16)
    for piece in range(PIECES):
        in_target[piece, :64, columns] = low[piece * 64 : piece * 64 + 64]
    low = out_grad.astype(BF16)
    for piece in range(PIECES // 2):
        place = half * (PIECES // 2) + piece
        out_target[place, start : start + 64, :] = low[piece * 64 : piece * 64 + 64]


def turn_kernel(
    info_ref, normed_ref, middle_ref, w0, w1, w2, w3, bias_out_ref, cotangent_ref, gain_ref,
    stream_ref, stat_ref, g0, g1, g2, g3, hidden_grad_ref, small_ref, grad_ref,
    total_ref, back_ref, low_ref, after,
):
    normed = normed_ref[...]
    following = ((w2,), (w3,), (middle_ref, bias_out_ref, gain_ref), after)

    def begin_grad(rows, totals):
        grad = jnp.where(valid_rows(info_ref, rows), cotangent_ref[0, rows, :].astype(F32), 0.0)
        low_ref[rows, :] = grad.astype(BF16)
        return (fold(totals[0], grad),)

    ready(cotangent_ref)
    (small_ref[2:3, :],) = by_rows(begin_grad, 1)
    grad_low = low_ref[...]
    total_ref[...] = jnp.zeros_like(total_ref)
    back_ref[...] = jnp.zeros_like(back_ref)
    for slot, weight in enumerate((w0, w1, w2, w3)):
        ready(weight)
        begin(*following[slot])
        target = (g0, g1, g2, g3)[slot]

        @pl.loop(0, 2)
        def _(half):
            columns, rows = halves(half)
            hidden = dot(normed, weight[:512, columns]) + weight[1024:1025, columns].astype(F32)
            act, slope = gelu_parts(hidden)
            act = act.astype(BF16)
            total_ref[...] += dot(act, weight[rows, :])
            hidden_grad = (dot_nt(grad_low, weight[rows, :]) * slope).astype(BF16)
            back_ref[...] += dot_nt(hidden_grad, weight[:512, columns])
            put_half(target, target, 64, half, dot_tn(normed, hidden_grad), dot_tn(act, grad_low))
            hidden_grad_ref[slot : slot + 1, columns] = jnp.sum(
                hidden_grad.astype(F32), axis=0, keepdims=True
            )

        target.flush()
    ready(middle_ref, bias_out_ref, gain_ref)

    def finish(rows, totals):
        stream, first = add_branch(
            info_ref, rows, totals[:2], total_ref, bias_out_ref[1:2, :], middle_ref
        )
        stream_ref[rows, :] = stream
        through, second = normalize_back(
            middle_ref[rows, :], gain_ref[1, 1:2, :], back_ref[rows, :], totals[2:]
        )
        grad = jnp.where(valid_rows(info_ref, rows), cotangent_ref[0, rows, :].astype(F32), 0.0) + through
        grad_ref[rows, :] = grad
        return first + second

    stat_ref[0:1, :], stat_ref[1:2, :], small_ref[0:1, :], small_ref[1:2, :] = by_rows(finish, 4)


def mix_back_kernel(
    info_ref, grad_ref, weights_ref, mixed_ref, inverse_ref, qkv_ref, ctx_ref,
    output_ref, local_ref, core_ref, diag_ref, far_ref,
    sum_ref, pair_ref, query_ref, context_ref, bias_ref, count_ref, spread_ref, spread_t_ref, step_ref,
):
    even = info_ref[1] == 1
    grad_low = grad_ref[...].astype(BF16)
    sum_ref[...] = dot_nt(grad_low, weights_ref[...])
    rows_grad = dot_tn(mixed_ref[...], grad_low).astype(BF16)
    for slot in range(SLOTS):
        for j in range(4):
            output_ref[slot, j * 128 : (j + 1) * 128, :] = rows_grad[
                slot * 128 : (slot + 1) * 128, j * 128 : (j + 1) * 128
            ]
    ready(mixed_ref, inverse_ref)

    def scale(rows, totals):
        scaled = sum_ref[rows, :].astype(BF16).astype(F32) * inverse_ref[rows, :]
        along = -scaled * mixed_ref[rows, :].astype(F32)
        for slot in range(SLOTS):
            columns = slice(slot * HEAD_PAIR, (slot + 1) * HEAD_PAIR)
            pair_ref[slot, rows, :HEAD_PAIR] = scaled[:, columns].astype(BF16)
            pair_ref[slot, rows, HEAD_PAIR:] = along[:, columns].astype(BF16)
        return totals

    by_rows(scale)
    for slot in range(SLOTS):
        pair_ref[slot, ROWS:, :] = dot(spread_t_ref[...], pair_ref[slot, :ROWS, :]).astype(BF16)

    output_ref.flush()
    ready(qkv_ref, ctx_ref)

    @pl.loop(0, SLOTS)
    def _(slot):
        held = None
        for query_row, context_row, keys, mask in TILES:
            queries = head_stack(qkv_ref[slot, query_row : query_row + TILE, :HEAD_PAIR])
            context = slice(context_row, context_row + keys)
            keyed = ctx_ref[slot, context, :HEAD_PAIR]
            scores = dot_nt(queries, keyed)
            weights = jnp.exp(scores + bias_ref[mask, :, :keys])
            values = jnp.concatenate(
                [ctx_ref[slot, context, HEAD_PAIR:], count_ref[context, :]], axis=1
            )
            upper = head_stack(pair_ref[slot, query_row : query_row + TILE, :])
            grad_scores = (dot_nt(upper, values) * weights).astype(BF16)
            query_ref[slot, query_row : query_row + TILE, :] = head_join(dot(grad_scores, keyed)) * 0.125
            key_part = dot_tn(grad_scores, queries)
            value_part = dot_tn(weights.astype(BF16), upper[:, :HEAD_PAIR])
            part = jnp.concatenate([key_part, value_part], axis=1)
            if context_row % TILE == 0 and context_row in (64, 128, 192) or context_row == 352:
                part = jnp.concatenate([part[:32] + held, part[32:]], axis=0)
            if context_row in (0, 64, 128, 288):
                held = part[TILE:]
                part = part[:TILE]
            context_ref[slot, context_row : context_row + part.shape[0], :] = part

    for slot in range(SLOTS):
        step_inv = step_ref[...]
        own = jnp.concatenate(
            [
                context_ref[slot, CTX_OWN[level] : CTX_OWN[level] + LEVEL_SIZE[level], :]
                for level in (1, 2, 3)
            ]
            + [jnp.zeros((32, 2 * HEAD_PAIR), F32)],
            axis=0,
        )
        coarse = jnp.concatenate(
            [query_ref[slot, ROWS:, :] * step_inv, own[:, :HEAD_PAIR] * step_inv, own[:, HEAD_PAIR:]],
            axis=1,
        ).astype(BF16)
        down = dot(spread_ref[...], coarse)
        local = query_ref[slot, :ROWS, :] + down[:, :HEAD_PAIR]
        local_ref[slot, :, :HEAD_PAIR] = local.astype(BF16)
        local = context_ref[slot, 16 : 16 + ROWS, :] + down[:, HEAD_PAIR:]
        local_ref[slot, :, HEAD_PAIR:] = local.astype(BF16)
        local_ref.flush_part(slot)
        for level in range(5):
            rows = slice(level * 16, level * 16 + 16)
            before = context_ref[slot, CTX_PREV[level] : CTX_PREV[level] + 16, :]
            after = context_ref[slot, CTX_NEXT[level] : CTX_NEXT[level] + 16, :]
            core_ref[slot, rows, :] = jnp.where(even, after, before).astype(BF16)
            diag_ref[slot, rows, :] = jnp.where(even, before, after).astype(BF16)
        diag_ref[slot, 80:96, :] = context_ref[slot, CTX_DIAG : CTX_DIAG + 16, :].astype(BF16)
        far_ref[slot, :, :] = context_ref[slot, CTX_Y : CTX_Y + 16, :].astype(BF16)
        for target in (core_ref, diag_ref, far_ref):
            target.flush_part(slot)


def back_tables(info_ref, bias_ref, count_ref, spread_ref, spread_t_ref, step_ref):
    fill_bias(bias_ref)
    fill_count(info_ref, count_ref)
    spread_ref[...] = spread_table()
    spread_t_ref[...] = spread_table(True)
    step_ref[...] = step_inverse()


def chained(body, inputs, outputs, scratch):
    def kernel(info_ref, *refs):
        refs = list(refs)
        parts = [[refs.pop(0) for _ in range(n)] for n in (inputs, 5, outputs, 5, scratch)]
        ins, back_ins, outs, back_outs, held = parts
        back_tables(info_ref, *refs[4:])
        body(info_ref, *ins, *outs, *held, tuple(back_ins))
        for result in outs:
            result.flush()
        mix_back_kernel(info_ref, outs[-1], *back_ins, *back_outs, *refs)

    return kernel


def project_back(
    info_ref, local_ref, core_ref, diag_ref, far_ref, normed, weights, targets, output_ref,
    low_ref, back_ref,
):
    keep = row_mask(info_ref, (ROWS, 3 * HEAD_PAIR))
    halo = halo_table(info_ref)
    scale = halo_step()
    for slot in range(SLOTS):
        arrived = jnp.concatenate(
            [core_ref[slot ^ 1, :, :], diag_ref[slot ^ 3, :, :], far_ref[slot ^ 2, :, :]], axis=0
        ).astype(F32)
        arrived = jnp.concatenate(
            [arrived[:, :HEAD_PAIR] * scale, arrived[:, HEAD_PAIR:]], axis=1
        ).astype(BF16)
        added = dot(halo, arrived)
        local = local_ref[slot, :, :].astype(F32)
        whole = jnp.concatenate([local[:, :HEAD_PAIR], local[:, HEAD_PAIR:] + added], axis=1)
        low_ref[:, slot * 384 : (slot + 1) * 384] = jnp.where(keep, whole, 0.0).astype(BF16)
    back_ref[...] = dot_nt(low_ref[...], weights[...])
    for slot in range(SLOTS):
        put_grads(targets[slot], 0, dot_tn(normed, low_ref[:, slot * 384 : (slot + 1) * 384]))
        put_grads(targets[slot], 0, output_ref[slot, :, :], 3 * HEAD_PAIR)


def between_kernel(
    info_ref, local_ref, core_ref, diag_ref, far_ref,
    normed_ref, projections, grad_in_ref, stream_ref, gain_ref,
    act_ref, slope_ref, second_ref, middle_ref, w0, w1, w2, w3, output_ref,
    a0, a1, a2, a3, g0, g1, g2, g3, o0, o1, o2, o3, hidden_grad_ref, small_ref, grad_ref,
    back_ref, mid_ref, low_ref, joint_ref, after,
):
    ready(local_ref, core_ref, diag_ref, far_ref, normed_ref, projections)
    begin(output_ref, grad_in_ref, stream_ref, gain_ref, w0, slope_ref, second_ref, act_ref)
    following = ((w2, middle_ref), (w3,), (), after)
    project_back(
        info_ref, local_ref, core_ref, diag_ref, far_ref,
        normed_ref[...], projections, (a0, a1, a2, a3), output_ref, joint_ref, back_ref,
    )
    for target in (a0, a1, a2, a3):
        target.flush()
    ready(grad_in_ref, stream_ref, gain_ref)

    def middle(rows, totals):
        through, first = normalize_back(
            stream_ref[rows, :], gain_ref[1, 0:1, :], back_ref[rows, :], totals[:2]
        )
        grad = grad_in_ref[rows, :] + through
        mid_ref[rows, :] = grad
        low = grad.astype(BF16)
        low_ref[rows, :] = low
        return first + (fold(totals[2], low.astype(F32)),)

    small_ref[0:1, :], small_ref[1:2, :], small_ref[4:5, :] = by_rows(middle, 3)
    grad_low = low_ref[...]
    second = second_ref[...]
    back_ref[...] = jnp.zeros_like(back_ref)
    ready(act_ref, slope_ref)
    begin(w1)
    for slot, weight in enumerate((w0, w1, w2, w3)):
        ready(weight)
        begin(*following[slot])
        in_target, out_target = (g0, g1, g2, g3)[slot], (o0, o1, o2, o3)[slot]

        @pl.loop(0, 2)
        def _(half):
            columns, rows = halves(half)
            slope = slope_ref[slot, :, columns].astype(F32)
            hidden_grad = (dot_nt(grad_low, weight[rows, :]) * slope).astype(BF16)
            back_ref[...] += dot_nt(hidden_grad, weight[:512, columns])
            put_half(
                in_target, out_target, 0, half, dot_tn(second, hidden_grad), dot_tn(act_ref[slot, :, columns], grad_low)
            )
            hidden_grad_ref[slot : slot + 1, columns] = jnp.sum(
                hidden_grad.astype(F32), axis=0, keepdims=True
            )

        in_target.flush()
        out_target.flush()
    ready(middle_ref)

    def finish(rows, totals):
        through, totals = normalize_back(
            middle_ref[rows, :], gain_ref[0, 1:2, :], back_ref[rows, :], totals
        )
        grad_ref[rows, :] = mid_ref[rows, :] + through
        return totals

    small_ref[2:3, :], small_ref[3:4, :] = by_rows(finish, 2)


def last_kernel(
    info_ref, local_ref, core_ref, diag_ref, far_ref,
    normed_ref, projections, grad_in_ref, stream_ref, gain_ref, output_ref,
    stat_a, stat_b, stat_c, stat_d, small_a, small_b, hidden_one, hidden_two,
    a0, a1, a2, a3, grad_ref,
    joint_ref, back_ref,
):
    targets = (a0, a1, a2, a3)
    ready(local_ref, core_ref, diag_ref, far_ref, normed_ref, projections)
    begin(
        output_ref, grad_in_ref, stream_ref, gain_ref, stat_a, stat_b, stat_c, stat_d, small_a, small_b,
        hidden_one, hidden_two,
    )
    project_back(
        info_ref, local_ref, core_ref, diag_ref, far_ref,
        normed_ref[...], projections, targets, output_ref, joint_ref, back_ref,
    )
    ready(grad_in_ref, stream_ref, gain_ref)

    def finish(rows, totals):
        through, totals = normalize_back(
            stream_ref[0, rows, :].astype(F32), gain_ref[0, 0:1, :], back_ref[rows, :], totals
        )
        grad_ref[rows, :] = grad_in_ref[rows, :] + through
        return totals

    gain_grad, offset_grad = by_rows(finish, 2)
    grad_ref.flush()
    position = lax.broadcasted_iota(jnp.int32, (1, WIDTH), 1)
    valid = jnp.where(position < jnp.minimum(info_ref[0], ROWS), 1.0, 0.0)
    lines = [
        gain_grad, offset_grad,
        small_b[0:1, :], small_b[1:2, :], small_b[2:3, :], small_b[3:4, :], small_b[4:5, :],
        small_a[0:1, :], small_a[1:2, :], small_a[2:3, :],
        stat_a[...], stat_b[0:1, :], stat_b[1:2, :], stat_c[...], stat_d[0:1, :], stat_d[1:2, :],
        valid,
    ]
    zero = jnp.zeros((1, WIDTH), F32)
    for slot in range(SLOTS):
        target = targets[slot]
        own = lines + [hidden_one[slot : slot + 1, :], hidden_two[slot : slot + 1, :]]
        own = own + [zero] * (8 * PIECES - len(own))
        for piece in range(PIECES):
            rows = jnp.concatenate(own[piece * 8 : piece * 8 + 8], axis=0)
            target[piece, 64:72, :] = rows.astype(BF16)


def far_sum_kernel(index_ref, keep_ref, arrived_ref, back_ref, stay_ref, go_ref):
    side = index_ref[0]
    for place in range(PIECES // 2):
        for target, which in ((stay_ref, side), (go_ref, 1 - side)):
            piece = 2 * place + which
            target[place] = (
                keep_ref[piece].astype(F32)
                + arrived_ref[piece].astype(F32)
                + back_ref[piece].astype(F32)
            ).astype(BF16)


def split_sum_kernel(bit, index_ref, stay_ref, arrived_ref, next_stay_ref, next_go_ref):
    side = index_ref[bit]
    for place in range(next_stay_ref.shape[0]):
        for target, which in ((next_stay_ref, side), (next_go_ref, 1 - side)):
            piece = 2 * place + which
            target[place] = (stay_ref[piece].astype(F32) + arrived_ref[piece].astype(F32)).astype(BF16)


def add_kernel(stay_ref, arrived_ref, sum_ref):
    sum_ref[...] = (stay_ref[...].astype(F32) + arrived_ref[...].astype(F32)).astype(BF16)


def join_kernel(bit, index_ref, own_ref, other_ref, block_ref):
    side = index_ref[bit]
    for place in range(own_ref.shape[0]):
        block_ref[2 * place + side] = own_ref[place]
        block_ref[2 * place + 1 - side] = other_ref[place]


def placed(info_ref, own, other):
    side = info_ref[3]
    for place in range(PIECES // 2):
        yield 2 * place + side, own, place
        yield 2 * place + 1 - side, other, place


def feed_result_kernel(
    info_ref, own_two, other_two, own_in, other_in, own_out, other_out, in_ref, out_ref
):
    ready(own_two, other_two, own_in, other_in, own_out, other_out)
    for layer, target, pair, start in (
        (1, in_ref, (own_two, other_two), 0), (1, out_ref, (own_two, other_two), 64),
        (0, in_ref, (own_in, other_in), 0), (0, out_ref, (own_out, other_out), 0),
    ):
        for piece, source, place in placed(info_ref, *pair):
            rows = pl.ds(pl.multiple_of(piece * 64, 64), 64)
            target[layer, rows, :] = source[place, start : start + 64, :].astype(F32)
        target.flush_part(layer)


def attn_result_kernel(
    info_ref, own_one, other_one, own_two, other_two,
    query_ref, key_ref, value_ref, output_ref, b_in_ref, gain_ref, offset_ref, b_out_ref, norm_ref,
    lines_ref,
):
    for layer, pair in ((1, (own_two, other_two)), (0, (own_one, other_one))):
        ready(*pair)
        for piece, source, place in placed(info_ref, *pair):
            rows = pl.ds(pl.multiple_of(piece * 64, 64), 64)
            part = source[place, :64, :].astype(F32)
            for i, target in enumerate((query_ref, key_ref, value_ref)):
                target[layer, rows, :] = part[:, i * HEAD_PAIR : (i + 1) * HEAD_PAIR]
            where = pl.ds(pl.multiple_of((piece % 2) * 64, 64), 64)
            columns = pl.ds(pl.multiple_of((piece // 2) * 128, 128), 128)
            output_ref[layer, where, columns] = part[:, 3 * HEAD_PAIR :]
            if layer == 0:
                rows = pl.ds(pl.multiple_of(piece * 8, 8), 8)
                lines_ref[rows, :] = source[place, 64:, :].astype(F32)
        for target in (query_ref, key_ref, value_ref, output_ref):
            target.flush_part(layer)
    for number, (target, place) in enumerate(
        (
            (gain_ref, (0, 0)), (offset_ref, (0, 0)), (gain_ref, (1, 0)), (offset_ref, (1, 0)),
            (gain_ref, (0, 1)), (offset_ref, (0, 1)), (b_out_ref, (0,)),
            (gain_ref, (1, 1)), (offset_ref, (1, 1)), (b_out_ref, (1,)),
        )
    ):
        line = lines_ref[number : number + 1, :]
        target[place[:-1] + (slice(place[-1], place[-1] + 1), slice(None))] = line
    b_in_ref[...] = lines_ref[17:19, :]
    squares = jnp.sum(lines_ref[10:18, :], axis=1, keepdims=True)
    count = jnp.sum(lines_ref[16:17, :], axis=1, keepdims=True)
    roots = jnp.sqrt(squares / (count * WIDTH))
    lane = iota((1, 128), 1)
    row = jnp.zeros((1, 128), F32)
    for i in range(3 * LAYERS):
        row = jnp.where(lane == i, roots[i : i + 1, :], row)
    norm_ref[...] = row[:, : 3 * LAYERS]


AFTER = []
ORDER = [None]


def in_order(value):
    before = [other for other in (ORDER[0], *AFTER) if other is not None]
    AFTER.clear()
    return tie(value, *before) if before else value


class Plan:
    def __init__(self, parts, dims, moves):
        self.parts, self.dims, self.moves = list(parts), dims, moves


def everything(value):
    return Plan([value], value.shape, [(0, None, None)])


def feed_plan(parts):
    if len(parts) == 1:
        return everything(parts[0])
    rows, width = parts[0].shape

    def half(number):
        def place(info_ref):
            side = info_ref[3] if number == 0 else 1 - info_ref[3]
            return pl.ds(pl.multiple_of(side * rows, 16), rows), slice(None)

        return place

    return Plan(parts, (2 * rows, width), [(i, None, half(i)) for i in range(2)])


def qkv_plan(slots):
    parts, moves = [], []
    for slot, group in enumerate(slots):
        rows = 512 // len(group)
        for i, part in enumerate(group):
            place = (slice(i * rows, (i + 1) * rows), slice(slot * 384, (slot + 1) * 384))
            moves.append((len(parts), (slice(None), slice(0, 384)), place))
            parts.append(part)
    return Plan(parts, (512, 384 * len(slots)), moves)


def output_plan(slots):
    parts, moves = [], []
    for slot, group in enumerate(slots):
        for j in range(4):
            rows = 4 // len(group)
            start = j % rows * 128
            source = (slice(start, start + 128), slice(384, 512))
            number = len(parts) + j // rows
            place = (slice(slot * 128, (slot + 1) * 128), slice(j * 128, (j + 1) * 128))
            moves.append((number, source, place))
        parts += group
    return Plan(parts, (512, 512), moves)


class Late:
    def __init__(self, arg):
        self.arg = arg


class Arriving:
    def __init__(self, ref, make, late):
        self.ref, self.make, self.copies = ref, make, None
        if not late:
            self.start()

    def start(self):
        if self.copies is None:
            self.copies = self.make()
            for copy in self.copies:
                copy.start()

    def wait(self):
        self.start()
        for copy in self.copies:
            copy.wait()
        self.copies = []

    def __getitem__(self, place):
        self.wait()
        return self.ref[place]


def begin(*arriving):
    for operand in arriving:
        operand.start()


class Leaving:
    def __init__(self, ref, target, sem):
        self.ref, self.target, self.sem, self.started = ref, target, sem, False
        self.copy = pltpu.make_async_copy(ref, target, sem)

    def flush(self):
        if not self.started:
            self.copy.start()
        self.started = True

    def flush_part(self, place):
        pltpu.make_async_copy(self.ref.at[place], self.target.at[place], self.sem).start()
        self.started = True

    def __getitem__(self, place):
        return self.ref[place]

    def __setitem__(self, place, value):
        self.ref[place] = value


def ready(*arriving):
    for operand in arriving:
        operand.wait()


def staged(body, name, out, args, scratch=(), flops=0):
    args = (in_order(args[0]),) + tuple(args[1:])
    late = [isinstance(arg, Late) for arg in args[1:]]
    plans = [arg.arg if isinstance(arg, Late) else arg for arg in args[1:]]
    plans = [plan if isinstance(plan, Plan) else everything(plan) for plan in plans]
    flat = [part for plan in plans for part in plan.parts]
    count = sum(len(plan.moves) for plan in plans)
    held = [pltpu.VMEM(plan.dims, plan.parts[0].dtype) for plan in plans]

    def kernel(*refs):
        info_ref, refs = refs[0], list(refs[1:])
        sources = [refs.pop(0) for _ in flat]
        targets = [refs.pop(0) for _ in out]
        inner = [refs.pop(0) for _ in held]
        outer = [refs.pop(0) for _ in out]
        sem_in = refs.pop()
        sem_out = refs.pop()
        arriving = []
        start, number = 0, 0
        for plan, ref, later in zip(plans, inner, late):

            def make(plan=plan, ref=ref, start=start, number=number):
                copies = []
                for i, (part, source_place, place) in enumerate(plan.moves):
                    source, target = sources[start + part], ref
                    if source_place is not None:
                        source = source.at[source_place]
                    if place is not None:
                        target = target.at[place(info_ref) if callable(place) else place]
                    copies.append(pltpu.make_async_copy(source, target, sem_in.at[number + i]))
                return copies

            arriving.append(Arriving(ref, make, later))
            start += len(plan.parts)
            number += len(plan.moves)
        leaving = [
            Leaving(ref, target, sem_out.at[i])
            for i, (ref, target) in enumerate(zip(outer, targets))
        ]
        body(info_ref, *arriving, *leaving, *refs)
        for operand in arriving:
            operand.wait()
        for result in leaving:
            result.flush()
        for result in leaving:
            result.copy.wait()

    result = pl.pallas_call(
        kernel,
        out_shape=tuple(out),
        in_specs=[pl.BlockSpec(memory_space=pltpu.SMEM)]
        + [pl.BlockSpec(memory_space=pl.ANY)] * len(flat),
        out_specs=tuple(pl.BlockSpec(memory_space=pl.ANY) for _ in out),
        scratch_shapes=held
        + [pltpu.VMEM(o.shape, o.dtype) for o in out]
        + list(scratch)
        + [pltpu.SemaphoreType.DMA((len(out),)), pltpu.SemaphoreType.DMA((count,))],
        cost_estimate=pl.CostEstimate(flops=1, bytes_accessed=1, transcendentals=0),
        name=name,
    )(args[0], *flat)
    ORDER[0] = result[-1]
    return result


def call(body, name, out, args, scalars=0):
    in_specs = [pl.BlockSpec(memory_space=pltpu.SMEM)] * scalars
    in_specs += [pl.BlockSpec(memory_space=pltpu.VMEM)] * (len(args) - scalars)
    args = (in_order(args[0]),) + tuple(args[1:])
    result = pl.pallas_call(
        body,
        out_shape=tuple(out),
        in_specs=in_specs,
        out_specs=tuple(pl.BlockSpec(memory_space=pltpu.VMEM) for _ in out),
        compiler_params=pltpu.CompilerParams(vmem_limit_bytes=4 << 20),
        cost_estimate=pl.CostEstimate(flops=1, bytes_accessed=1, transcendentals=0),
        name=name,
    )(*args)
    ORDER[0] = result[-1]
    return result


def start_attn(layer, wq, wk, wv, wo, block, sems):
    copies = []
    for i, source in enumerate((wq, wk, wv)):
        target = block.at[:, i * HEAD_PAIR : (i + 1) * HEAD_PAIR]
        copies.append(pltpu.make_async_copy(source.at[layer], target, sems.at[i]))
    for j in range(4):
        target = block.at[j * 128 : (j + 1) * 128, 3 * HEAD_PAIR :]
        source = wo.at[layer, :, j * 128 : (j + 1) * 128]
        copies.append(pltpu.make_async_copy(source, target, sems.at[3 + j]))
    for copy in copies:
        copy.start()
    return copies


def pack_first_kernel(wq, wk, wv, wo, own_ref, block, sems):
    for copy in start_attn(0, wq, wk, wv, wo, block, sems):
        copy.wait()
    copy = pltpu.make_async_copy(block, own_ref, sems.at[0])
    copy.start()
    copy.wait()


def pack_rest_kernel(
    info_ref, wq, wk, wv, wo, w_in, b_in, w_out,
    attn_two, feed_one, half_one, feed_two, half_two,
    attn, feeds, biases, sems, feed_sems, out_sems,
):
    side = info_ref[3]
    attn_copies = start_attn(1, wq, wk, wv, wo, attn, sems)
    feed_copies = []
    for layer in range(LAYERS):
        for i, source in enumerate((w_in, w_out)):
            copy = pltpu.make_async_copy(
                source.at[layer], feeds.at[layer, i * 512 : i * 512 + 512], feed_sems.at[layer * 2 + i]
            )
            copy.start()
            feed_copies.append(copy)
    bias_copy = pltpu.make_async_copy(b_in, biases, feed_sems.at[4])
    bias_copy.start()
    bias_copy.wait()
    row = iota((32, WIDTH), 0)
    for layer in range(LAYERS):
        line = jnp.broadcast_to(biases[layer : layer + 1, :].astype(F32), (32, WIDTH))
        feeds[layer, 1024:1056, :] = jnp.where(row == 0, line, 0.0).astype(BF16)
    place = pl.ds(pl.multiple_of(side * 528, 16), 528)
    sent = []
    for copies, parts in (
        (feed_copies[:2], [(feeds.at[0, place], half_one), (feeds.at[0], feed_one)]),
        (attn_copies, [(attn, attn_two)]),
        (feed_copies[2:], [(feeds.at[1, place], half_two), (feeds.at[1], feed_two)]),
    ):
        for copy in copies:
            copy.wait()
        for source, target in parts:
            sent.append(pltpu.make_async_copy(source, target, out_sems.at[len(sent)]))
            sent[-1].start()
    for copy in sent:
        copy.wait()


def pack_first(weights):
    return pl.pallas_call(
        pack_first_kernel,
        out_shape=shape((512, 512), BF16),
        in_specs=[pl.BlockSpec(memory_space=pl.ANY)] * 4,
        out_specs=pl.BlockSpec(memory_space=pl.ANY),
        scratch_shapes=[pltpu.VMEM((512, 512), BF16), pltpu.SemaphoreType.DMA((7,))],
        name="pack_first",
    )(*weights)


def pack_rest(info, weights):
    out = [(512, 512), (1056, 512), (528, 512), (1056, 512), (528, 512)]
    return pl.pallas_call(
        pack_rest_kernel,
        out_shape=tuple(shape(dims, BF16) for dims in out),
        in_specs=[pl.BlockSpec(memory_space=pltpu.SMEM)] + [pl.BlockSpec(memory_space=pl.ANY)] * 7,
        out_specs=tuple([pl.BlockSpec(memory_space=pl.ANY)] * 5),
        scratch_shapes=[
            pltpu.VMEM((512, 512), BF16),
            pltpu.VMEM((2, 1056, 512), BF16), pltpu.VMEM((2, 512), BF16),
            pltpu.SemaphoreType.DMA((7,)), pltpu.SemaphoreType.DMA((5,)), pltpu.SemaphoreType.DMA((5,)),
        ],
        name="pack_rest",
    )(info, *weights)


def shape(dims, dtype):
    return jax.ShapeDtypeStruct(dims, dtype)


def swap(value, axis, bit):
    size = lax.axis_size(axis)
    return lax.ppermute(value, axis, [(i, i ^ bit) for i in range(size)])


def halo_swap(core, diag, far):
    return swap(core, "tensor", 1), swap(diag, "tensor", 3), swap(far, "tensor", 2)


def tie(value, *others):
    return lax.optimization_barrier((value, *others))[0]


def far_sum(index, slots, arrived, back):
    pieces, rows = back.shape[:2]
    half = [shape((pieces // 2, rows, WIDTH), BF16)] * 2
    return call(far_sum_kernel, "far_sum", half, (index, slots[0], arrived[0], back), 1)


def core_swap(slots):
    far = swap(slots[3], "tensor", 1)
    return swap(slots[1], "tensor", 1), far


def core_sum(slots, arrived):
    return call(add_kernel, "core_sum", [shape(slots[2].shape, BF16)], (slots[2], arrived[1]))[0]


class Chain:
    def __init__(self, index, stay, go):
        self.index, self.stay, self.at = index, stay, 0
        self.arriving = swap(go, "dp", 1)

    def step(self):
        rest = self.stay.shape[1:]
        pieces = self.stay.shape[0]
        if self.at == 0:
            half = shape((pieces // 2,) + rest, BF16)
            self.stay, go = call(
                functools.partial(split_sum_kernel, 1), "split_sum", [half] * 2,
                (self.index, self.stay, self.arriving), 1,
            )
            self.arriving = swap(go, "dp", 2)
        elif self.at < 3:
            self.stay = call(
                add_kernel, "add", [shape(self.stay.shape, BF16)], (self.stay, self.arriving)
            )[0]
            if self.at == 2:
                bit = PIECES
                while bit < lax.axis_size("dp"):
                    self.stay = self.stay + swap(self.stay, "dp", bit)
                    bit *= 2
            self.arriving = swap(self.stay, "dp", 4 if self.at == 1 else 2)
        else:
            self.stay = call(
                functools.partial(join_kernel, 1), "join", [shape((pieces * 2,) + rest, BF16)],
                (self.index, self.stay, self.arriving), 1,
            )[0]
            self.arriving = swap(self.stay, "dp", 1)
        self.at += 1

    def result(self):
        assert self.at == 4
        return self.stay, self.arriving


class Flow:
    def __init__(self, index, slots, arrived, back=None, halos=()):
        self.index, self.slots, self.arrived, self.halos = index, slots, arrived, halos
        self.back, self.chain, self.at = back, None, 0 if back is None else 1

    def step(self):
        if self.at == 0:
            far = core_sum(self.slots, self.arrived)
            self.back = swap(tie(far, *self.halos) if self.halos else far, "tensor", 2)
        elif self.at == 1:
            self.chain = Chain(self.index, *far_sum(self.index, self.slots, self.arrived, self.back))
        elif self.at < 6:
            self.chain.step()
        else:
            AFTER.append(self.chain.arriving)
        self.at += 1


def on_device(
    inputs, lengths, cotangent, ln_gains, ln_biases,
    w_query, w_key, w_value, w_output, w_in, b_in, w_out, b_out,
):
    assert inputs.shape == (1, ROWS, WIDTH)
    assert lax.axis_size("tensor") == SLOTS and lax.axis_size("dp") % PIECES == 0
    rank = lax.axis_index("tensor")
    position = lax.axis_index("dp")
    side = position % 2
    index = jnp.stack([side, position // 2 % 2, position // 4 % 2]).astype(jnp.int32)
    near = (rank == 1) | (rank == 2)
    length = lengths[0]
    info = jnp.stack(
        [length - rank * ROWS, 1 - rank % 2, near.astype(jnp.int32), side, rank]
    ).astype(jnp.int32)

    def later(*values):
        return [Late(value) for value in values]

    ORDER[0] = None
    AFTER.clear()
    attn_own = pack_first((w_query, w_key, w_value, w_output))
    attn_two, feed_one, feed_one_half, feed_two, feed_two_half = pack_rest(
        tie(info, attn_own), (w_query, w_key, w_value, w_output, w_in, b_in, w_out)
    )
    own_far = swap(attn_own, "tensor", 2)
    own_core = swap(attn_own, "tensor", 1)
    slots = ((attn_own,), (own_core,))
    here_f1 = swap(feed_one_half, "tensor", 2)
    core_w = [swap(tie(own, own_core), "tensor", 1) for own in (feed_one, attn_two, feed_two)]

    qkv_shapes = [
        shape((SLOTS, 512, 384), BF16),
        shape((SLOTS, 80, 256), BF16),
        shape((SLOTS, 96, 256), BF16),
        shape((SLOTS, 16, 256), BF16),
    ]
    block_f32 = shape((ROWS, WIDTH), F32)
    block_low = shape((ROWS, WIDTH), BF16)

    sums = pltpu.VMEM((ROWS, WIDTH), F32)
    tables = [
        pltpu.VMEM((3, 128, 128), F32), pltpu.VMEM((CTX, 128), BF16), pltpu.VMEM((ROWS, ROWS), BF16)
    ]

    def mix(layer, qkv, halos, stream):
        return staged(
            functools.partial(mix_kernel, layer), "mix",
            [
                shape((SLOTS, CTX, 256), BF16), block_low, block_f32, block_f32, block_low, shape((1, WIDTH), F32),
            ],
            (
                info, qkv, *halos,
                *later(stream, ln_gains, ln_biases, output_weights[layer]),
            ),
            [pltpu.VMEM((SLOTS, 512, 256), F32), sums] + tables,
        )

    def with_mix_back(layer, body, name, out, args, held, saved, qkv):
        ctx, mixed, inverse = saved
        result = staged(
            chained(body, len(args), len(out), len(held)), name,
            list(out)
            + [
                shape((SLOTS, 512, 128), BF16),
                shape((SLOTS, ROWS, 384), BF16), shape((SLOTS, 80, 256), BF16),
                shape((SLOTS, 96, 256), BF16), shape((SLOTS, 16, 256), BF16),
            ],
            (info, *args, *later(output_weights[layer], mixed, inverse, qkv, ctx)),
            list(held)
            + [
                sums, pltpu.VMEM((SLOTS, 512, 256), BF16), pltpu.VMEM((SLOTS, 512, 128), F32),
                pltpu.VMEM((SLOTS, CTX, 256), F32),
            ]
            + tables
            + [pltpu.VMEM((ROWS, ROWS), BF16), pltpu.VMEM((ROWS, 128), F32)],
        )
        return result[: len(out)], result[len(out) :]

    near_shapes = [shape((2,) + dims.shape[1:], BF16) for dims in qkv_shapes]
    normed_one, stream_one, qkv_near, *pay_near = staged(
        first_near_kernel, "first_near", [block_low, block_f32] + near_shapes,
        (tie(info, feed_one_half), inputs, ln_gains, ln_biases, qkv_plan(slots[:2])),
    )
    own_diag = tuple(
        swap(part, "tensor", 1)
        for part in (tie(own_far, normed_one)[i * 256 : i * 256 + 256] for i in range(2))
    )
    slots += ((own_far,), own_diag)
    qkv_weights, output_weights = [qkv_plan(slots)], [output_plan(slots)]
    qkv_far, *pay = staged(
        first_kernel, "first", near_shapes[:1] + qkv_shapes[1:],
        (info, normed_one, qkv_plan(slots[2:]), *pay_near),
        [pltpu.VMEM(dims.shape, BF16) for dims in near_shapes[1:]],
    )
    qkv_one = Plan(
        (qkv_near, qkv_far), (SLOTS, 512, 384),
        [(0, None, (slice(0, 2),)), (1, None, (slice(2, 4),))],
    )
    halos = halo_swap(*pay)
    there_f1 = swap(tie(here_f1, halos[0]), "dp", 1)
    diag_f1 = swap(tie(here_f1, halos[0]), "tensor", 1)
    far_a2 = swap(tie(attn_two, here_f1, *halos), "tensor", 2)
    *saved_one, middle_one, second_one, stat_a = mix(0, qkv_one, halos, stream_one)
    here_f2 = swap(tie(feed_two_half, here_f1, stat_a), "tensor", 2)
    feed_weights = [[
        feed_plan(parts)
        for parts in (
            (feed_one,), (core_w[0],), (here_f1, there_f1),
            (diag_f1, swap(tie(there_f1, stat_a), "tensor", 1)),
        )
    ]]
    hidden = shape((SLOTS // 2, ROWS, 512), BF16)
    act_near, slope_near, total_near = staged(
        feed_near_kernel, "feed_near", [hidden, hidden, block_f32],
        (info, second_one, *feed_weights[0][:2]),
    )
    slots = (
        (attn_two,), (core_w[1],), (far_a2,), (swap(tie(far_a2, total_near), "tensor", 1),)
    )
    qkv_weights.append(qkv_plan(slots))
    output_weights.append(output_plan(slots))
    act_far, slope_far, stat_b, stream, normed_two, qkv_two, *pay = staged(
        feed_kernel, "feed",
        [hidden, hidden, shape((2, WIDTH), F32), block_f32, block_low] + qkv_shapes,
        (
            info, second_one, Late(middle_one), *feed_weights[0][2:],
            *later(total_near, b_out, ln_gains, ln_biases, qkv_weights[1]),
        ),
        [sums],
    )
    act, slope = (
        Plan(
            pair, (SLOTS, ROWS, 512),
            [(0, None, (slice(0, 2),)), (1, None, (slice(2, 4),))],
        )
        for pair in ((act_near, act_far), (slope_near, slope_far))
    )
    there_f2 = swap(tie(here_f2, there_f1, stat_b), "dp", 1)
    diag_f2 = swap(tie(here_f2, there_f1, stat_b), "tensor", 1)
    halos = halo_swap(*pay)
    *saved_two, middle_two, second_two, stat_c = mix(1, qkv_two, halos, stream)

    feed_weights.append([
        feed_plan(parts)
        for parts in (
            (feed_two,), (core_w[2],), (here_f2, there_f2),
            (diag_f2, swap(tie(there_f2, stat_c), "tensor", 1)),
        )
    ])

    def grads(matrices, extra=0):
        return [shape((PIECES, 64 * matrices + extra, WIDTH), BF16)] * SLOTS

    (result, stat_d, *f2, hidden_two, small_a, grad), (output_two, local, *pay) = with_mix_back(
        1, turn_kernel, "turn",
        [block_f32, shape((2, WIDTH), F32)] + grads(2)
        + [shape((SLOTS, WIDTH), F32), shape((3, WIDTH), F32), block_f32],
        (
            second_two, Late(middle_two), *feed_weights[1][:2], *later(*feed_weights[1][2:]),
            Late(b_out), cotangent, Late(ln_gains),
        ),
        [sums] * 2 + [pltpu.VMEM((ROWS, WIDTH), BF16)], saved_two, qkv_two,
    )
    halos = halo_swap(*pay)
    core_f2 = core_swap(f2)
    back_f2 = swap(tie(core_sum(f2, core_f2), *halos), "tensor", 2)
    (*both, hidden_one, small_b, grad), (output_one, local, *pay) = with_mix_back(
        0, between_kernel, "between",
        grads(1) * 3 + [shape((SLOTS, WIDTH), F32), shape((5, WIDTH), F32), block_f32],
        (
            local, *halos, normed_two, qkv_weights[1],
            *later(
                grad, stream, ln_gains, act, slope, second_one, middle_one, *feed_weights[0], output_two
            ),
        ),
        [sums] * 2 + [pltpu.VMEM((ROWS, WIDTH), BF16), pltpu.VMEM((ROWS, 384 * SLOTS), BF16)],
        saved_one, qkv_one,
    )
    a2, f1, g1 = both[:SLOTS], both[SLOTS : 2 * SLOTS], both[2 * SLOTS :]
    pay = [tie(part, back_f2) for part in pay]
    halos = halo_swap(*pay)
    core_f1 = core_swap(f1)
    core_a2 = core_swap(a2)
    core_g1 = core_swap(g1)
    f2 = Flow(index, f2, core_f2, back_f2)
    f1 = Flow(index, f1, core_f1, halos=halos)
    a2 = Flow(index, a2, core_a2, halos=halos)
    g1 = Flow(index, g1, core_g1, halos=halos)
    for flow in (f2, g1,):
        flow.step()
    *a1, input_grad = staged(
        last_kernel, "last",
        grads(1, 8) + [block_f32],
        (
            info, local, *halos, normed_one, qkv_weights[0],
            *later(
                grad, inputs, ln_gains, output_one, stat_a, stat_b, stat_c, stat_d, small_a, small_b,
                hidden_one, hidden_two,
            ),
        ),
        [pltpu.VMEM((ROWS, 384 * SLOTS), BF16), sums],
    )
    a1 = Flow(index, a1, core_swap(a1))
    for flow in (
        f1, f2, g1, a1, f2, g1, f1, a2, a1, f1, g1, f2,
        f1, a2, a1, f2, f1, a2, a1, g1, f1, a2, a1, g1,
        f2, f1, a2, a1, g1,
    ):
        flow.step()
    a2.step()
    grad_in, grad_out = staged(
        feed_result_kernel, "feed_result", [shape((2, 512, 512), F32)] * 2,
        (info, *f2.chain.result(), *f1.chain.result(), *g1.chain.result()),
    )
    a1.step()
    a2.step()
    (
        grad_query, grad_key, grad_value, grad_output, grad_b_in, gains, offsets, grad_b_out, norms
    ) = staged(
        attn_result_kernel, "attn_result",
        [shape((2, 512, 128), F32)] * 3
        + [
            shape((2, 128, 512), F32), shape((2, 512), F32), shape((2, 2, 512), F32),
            shape((2, 2, 512), F32), shape((2, 512), F32), shape((1, 3 * LAYERS), F32),
        ],
        (info, *a1.chain.result(), *a2.chain.result()),
        [pltpu.VMEM((8 * PIECES, WIDTH), F32)],
    )
    return (
        result[None], input_grad[None], gains, offsets,
        grad_query, grad_key, grad_value, grad_output, grad_in, grad_b_in, grad_out,
        grad_b_out, norms.reshape(3 * LAYERS),
    )


def solution(mesh):
    return jax.shard_map(
        on_device,
        mesh=mesh,
        in_specs=(
            P("dp", "tensor", None),
            P("dp"),
            P("dp", "tensor", None),
            P(),
            P(),
            P(None, None, "tensor"),
            P(None, None, "tensor"),
            P(None, None, "tensor"),
            P(None, "tensor", None),
            P(None, None, "tensor"),
            P(None, "tensor"),
            P(None, "tensor", None),
            P(),
        ),
        out_specs=(
            P("dp", "tensor", None),
            P("dp", "tensor", None),
            P(),
            P(),
            P(None, None, "tensor"),
            P(None, None, "tensor"),
            P(None, None, "tensor"),
            P(None, "tensor", None),
            P(None, None, "tensor"),
            P(None, "tensor"),
            P(None, "tensor", None),
            P(),
            P(),
        ),
        check_vma=False,
    )
```

profile of v0, /device:TPU:0, one launch (start us, length us, event | category | flops | bytes accessed | tf_op | source)
XLA Modules:
  0.0 259.3 jit_solution(10325960026126831925)
XLA Ops:
  0.6 1.9 pack_first.1.refs_4_.refs_9_.refs_26_.refs_6_
  3.1 2.6 collective-permute-start.1
  6.9 4.3 %pack_rest.1 = (bf16[512,512]{1,0:T(8,128)(2,1)}, bf16[1056,512]{1,0:T(8,128)(2,1)}, bf16[528,512]{1,0:T(8,128)(2,1)}, bf16[1056,512]{1,0:T(8,128)(2,1)}, bf16[528,512]{1,0:T(8,128)(2,1)}) custom-call(s32[5]{0:T(128)} %stack.37.info_ref.refs_0_, bf16[2,512,128]{2,1,0:T(8,128)(2,1)} %wq.3, bf16[2,512,128]{2,1,0:T(8,128)(2,1)} %wk.3, bf16[2,512,128]{2,1,0:T(8,128)(2,1)} %wv.3, ...), custom_call_target="tpu_custom_call" | custom-call | tf_op jit(solution)/shard_map/pack_rest/pallas_call | solution.py:1092
  12.1 3.7 %first_near.1 = (bf16[256,512]{1,0:T(8,128)(2,1)}, f32[256,512]{1,0:T(8,128)}, bf16[2,512,384]{2,1,0:T(8,128)(2,1)}, bf16[2,80,256]{2,1,0:T(8,128)(2,1)}, bf16[2...) custom-call(s32[5]{0:T(128)} %stack.37.info_ref.refs_0_, bf16[1,256,512]{2,1,0:T(8,128)(2,1)} %refs_12_.3, ...), custom_call_target="tpu_custom_call" | custom-call | flops 1 | bytes 1 | tf_op jit(solution)/shard_map/first_near/pallas_call | solution.py:985
  15.8 2.9 %collective-permute-done.1.refs_2_.refs_11_.refs_28_.refs_8_ = bf16[512,512]{1,0:T(8,128)(2,1)S(1)} collective-permute-done((bf16[512,512]{1,0:T(8,128)(2,1)}, bf16[512,512]{1,0:T(8,128)(2,1)S(1)}, u32[]{:S(2)}, u32[]{:S(2)}) %collective-permute-start.1) | collective-permute-done | bytes 524320 | tf_op jit(solution)/shard_map/ppermute | solution.py:1112
  21.4 3.7 %first.1 = (bf16[2,512,384]{2,1,0:T(8,128)(2,1)}, bf16[4,80,256]{2,1,0:T(8,128)(2,1)}, bf16[4,96,256]{2,1,0:T(8,128)(2,1)}, bf16[4,16,256]{2,1,0:T(8,128)(2,1)}) custom-call(s32[5]{0:T(128)} %stack.37.info_ref.refs_0_, bf16[256,512]{1,0:T(8,128)(2,1)} %get-tuple-element.187.refs_1_.refs_5_, bf16[512,512]{1,0:T(8,128)(2,1)} %copy-done.17, ...), custom_call_target="tpu_custom_call" | custom-call | flops 1 | bytes 1 | tf_op jit(solution)/shard_map/first/pallas_call | solution.py:985
  25.0 1.8 collective-permute-start.5
  27.3 3.1 %collective-permute-done.8.refs_3_.refs_21_ = bf16[528,512]{1,0:T(8,128)(2,1)} collective-permute-done((bf16[528,512]{1,0:T(8,128)(2,1)}, bf16[528,512]{1,0:T(8,128)(2,1)}, u32[]{:S(2)}, u32[]{:S(2)}) %collective-permute-start.8) | collective-permute-done | bytes 540704 | tf_op jit(solution)/shard_map/ppermute | solution.py:1112
  30.3 1.9 collective-permute-start.9
  32.3 2.6 %collective-permute-done.6.refs_5_ = bf16[4,16,256]{2,1,0:T(8,128)(2,1)S(1)} collective-permute-done((bf16[4,16,256]{2,1,0:T(8,128)(2,1)}, bf16[4,16,256]{2,1,0:T(8,128)(2,1)S(1)}, u32[]{:S(2)}, u32[]{:S(2)}) %collective-permute-start.6) | collective-permute-done | bytes 32800 | tf_op jit(solution)/shard_map/ppermute | solution.py:1112
  34.9 1.8 collective-permute-start.13
  36.7 7.9 %mix.2 = (bf16[4,672,256]{2,1,0:T(8,128)(2,1)}, bf16[256,512]{1,0:T(8,128)(2,1)}, f32[256,512]{1,0:T(8,128)}, f32[256,512]{1,0:T(8,128)}, bf16[256,512]{1,0:T(8,128)(2,1)}, /*index=5*/f32[1,512]{1,0:T(1,128)}) custom-call(s32[5]{0:T(128)} %stack.37.info_ref.refs_0_, bf16[2,512,384]{2,1,0:T(8,128)(2,1)} %get-tuple-element.193.refs_1_.refs_33_, ...), custom_call_target="tpu_custom_call" | custom-call | flops 1 | bytes 1 | tf_op jit(solution)/shard_map/mix/pallas_call | solution.py:985
  46.9 4.5 %feed_near.1 = (bf16[2,256,512]{2,1,0:T(8,128)(2,1)}, bf16[2,256,512]{2,1,0:T(8,128)(2,1)}, f32[256,512]{1,0:T(8,128)}) custom-call(s32[5]{0:T(128)} %stack.37.info_ref.refs_0_, bf16[256,512]{1,0:T(8,128)(2,1)} %get-tuple-element.200.refs_1_.refs_17_, bf16[1056,512]{1,0:T(8,128)(2,1)} %get-tuple-element.202.refs_2_.refs_19_, bf16[1056,512]{1,0:T(8,128)(2,1)} %copy-done.23), custom_call_target="tpu_custom_call" | custom-call | flops 1 | bytes 1 | tf_op jit(solution)/shard_map/feed_near/pallas_call | solution.py:985
  51.8 1.7 collective-permute-done.14.refs_14_.refs_11_.refs_15_.refs_9_
  54.3 7.0 %feed.1 = (bf16[2,256,512]{2,1,0:T(8,128)(2,1)}, bf16[2,256,512]{2,1,0:T(8,128)(2,1)}, f32[2,512]{1,0:T(2,128)}, f32[256,512]{1,0:T(8,128)}, bf16[256,512]{1,0:T...) custom-call(s32[5]{0:T(128)} %stack.37.info_ref.refs_0_, ...), custom_call_target="tpu_custom_call" | custom-call | flops 1 | bytes 1 | tf_op jit(solution)/shard_map/feed/pallas_call | solution.py:985
  61.3 1.6 collective-permute-start.20
  62.8 1.4 collective-permute-start.16
  65.0 6.0 %collective-permute-done.17.refs_4_ = bf16[4,16,256]{2,1,0:T(8,128)(2,1)S(1)} collective-permute-done((bf16[4,16,256]{2,1,0:T(8,128)(2,1)}, bf16[4,16,256]{2,1,0:T(8,128)(2,1)S(1)}, u32[]{:S(2)}, u32[]{:S(2)}) %collective-permute-start.17) | collective-permute-done | bytes 32800 | tf_op jit(solution)/shard_map/ppermute | solution.py:1112
  71.7 7.7 %mix.3 = (bf16[4,672,256]{2,1,0:T(8,128)(2,1)}, bf16[256,512]{1,0:T(8,128)(2,1)}, f32[256,512]{1,0:T(8,128)}, f32[256,512]{1,0:T(8,128)}, bf16[256,512]{1,0:T(8,128)(2,1)}, /*index=5*/f32[1,512]{1,0:T(1,128)}) custom-call(s32[5]{0:T(128)} %stack.37.info_ref.refs_0_, bf16[4,512,384]{2,1,0:T(8,128)(2,1)} %get-tuple-element.214.refs_1_.refs_18_, ...), custom_call_target="tpu_custom_call" | custom-call | flops 1 | bytes 1 | tf_op jit(solution)/shard_map/mix/pallas_call | solution.py:985
  80.0 1.5 collective-permute-done.22.refs_8_
  82.3 21.5 %turn.1 = (f32[256,512]{1,0:T(8,128)}, f32[2,512]{1,0:T(2,128)}, bf16[8,128,512]{2,1,0:T(8,128)(2,1)}, bf16[8,128,512]{2,1,0:T(8,128)(2,1)}, bf16[8,128,512]{2,1...) custom-call(s32[5]{0:T(128)} %stack.37.info_ref.refs_0_, ...), custom_call_target="tpu_custom_call" | custom-call | flops 1 | bytes 1 | tf_op jit(solution)/shard_map/turn/pallas_call | solution.py:985
  104.3 1.1 collective-permute-start.25
  106.8 1.2 copy-done.2
  108.3 4.1 %collective-permute-done.26.refs_4_ = bf16[4,16,256]{2,1,0:T(8,128)(2,1)S(1)} collective-permute-done((bf16[4,16,256]{2,1,0:T(8,128)(2,1)}, bf16[4,16,256]{2,1,0:T(8,128)(2,1)S(1)}, u32[]{:S(2)}, u32[]{:S(2)}) %collective-permute-start.26) | collective-permute-done | bytes 32800 | tf_op jit(solution)/shard_map/ppermute | solution.py:1112
  112.4 1.4 collective-permute-start.28
  113.8 22.3 %between.1 = (bf16[8,64,512]{2,1,0:T(8,128)(2,1)}, bf16[8,64,512]{2,1,0:T(8,128)(2,1)}, bf16[8,64,512]{2,1,0:T(8,128)(2,1)}, bf16[8,64,512]{2,1,0:T(8,128)(2,1)}...) custom-call(s32[5]{0:T(128)} %stack.37.info_ref.refs_0_, ...), custom_call_target="tpu_custom_call" | custom-call | flops 1 | bytes 1 | tf_op jit(solution)/shard_map/between/pallas_call | solution.py:985
  137.3 1.4 collective-permute-start.31
  138.9 2.4 far_sum.5
  143.3 1.2 core_sum.6
  144.5 2.0 collective-permute-done.32.refs_4_
  147.4 6.5 %last.1 = (bf16[8,72,512]{2,1,0:T(8,128)(2,1)}, bf16[8,72,512]{2,1,0:T(8,128)(2,1)}, bf16[8,72,512]{2,1,0:T(8,128)(2,1)}, bf16[8,72,512]{2,1,0:T(8,128)(2,1)}, f32[256,512]{1,0:T(8,128)}) custom-call(s32[5]{0:T(128)} %stack.37.info_ref.refs_0_, bf16[4,256,384]{2,1,0:T(8,128)(2,1)} %get-tuple-element.261.refs_1_, bf16[4,80,256]{2,1,0:T(8,128)(2,1)} %copy-done.41, ...), custom_call_target="tpu_custom_call" | custom-call | flops 1 | bytes 1 | tf_op jit(solution)/shard_map/last/pallas_call | solution.py:985
  154.6 2.0 collective-permute-done.34.arrived_ref
  157.3 1.6 collective-permute-start.38
  158.9 2.0 collective-permute-done.36.back_ref
  161.7 1.6 collective-permute-start.39
  163.8 1.4 collective-permute-done.38.arrived_ref
  166.1 3.6 %collective-permute-done.39.arrived_ref = bf16[4,64,512]{2,1,0:T(8,128)(2,1)S(1)} collective-permute-done((bf16[4,64,512]{2,1,0:T(8,128)(2,1)S(1)}, bf16[4,64,512]{2,1,0:T(8,128)(2,1)S(1)}, u32[]{:S(2)}, u32[]{:S(2)}) %collective-permute-start.39) | collective-permute-done | bytes 262176 | tf_op jit(solution)/shard_map/ppermute | solution.py:1112
  171.1 9.0 %collective-permute-done.41.back_ref = bf16[8,64,512]{2,1,0:T(8,128)(2,1)S(1)} collective-permute-done((bf16[8,64,512]{2,1,0:T(8,128)(2,1)S(1)}, bf16[8,64,512]{2,1,0:T(8,128)(2,1)S(1)}, u32[]{:S(2)}, u32[]{:S(2)}) %collective-permute-start.41) | collective-permute-done | bytes 524320 | tf_op jit(solution)/shard_map/ppermute | solution.py:1112
  181.6 1.2 collective-permute-start.50
  182.8 2.6 collective-permute-start.47
  185.4 7.4 %collective-permute-done.44.back_ref = bf16[8,72,512]{2,1,0:T(8,128)(2,1)S(1)} collective-permute-done((bf16[8,72,512]{2,1,0:T(8,128)(2,1)S(1)}, bf16[8,72,512]{2,1,0:T(8,128)(2,1)S(1)}, u32[]{:S(2)}, u32[]{:S(2)}) %collective-permute-start.44) | collective-permute-done | bytes 589856 | tf_op jit(solution)/shard_map/ppermute | solution.py:1112
  192.7 1.6 collective-permute-start.46
  196.3 2.8 %collective-permute-done.46.arrived_ref = bf16[2,64,512]{2,1,0:T(8,128)(2,1)S(1)} collective-permute-done((bf16[2,64,512]{2,1,0:T(8,128)(2,1)S(1)}, bf16[2,64,512]{2,1,0:T(8,128)(2,1)S(1)}, u32[]{:S(2)}, u32[]{:S(2)}) %collective-permute-start.46) | collective-permute-done | bytes 131104 | tf_op jit(solution)/shard_map/ppermute | solution.py:1112
  199.5 1.9 collective-permute-start.48
  201.4 6.9 %collective-permute-done.48.arrived_ref = bf16[2,64,512]{2,1,0:T(8,128)(2,1)S(1)} collective-permute-done((bf16[2,64,512]{2,1,0:T(8,128)(2,1)S(1)}, bf16[2,64,512]{2,1,0:T(8,128)(2,1)S(1)}, u32[]{:S(2)}, u32[]{:S(2)}) %collective-permute-start.48) | collective-permute-done | bytes 131104 | tf_op jit(solution)/shard_map/ppermute | solution.py:1112
  209.1 1.1 collective-permute-start.54
  210.2 3.0 %collective-permute-start.53 = (bf16[2,64,512]{2,1,0:T(8,128)(2,1)S(1)}, bf16[2,64,512]{2,1,0:T(8,128)(2,1)S(1)}, u32[]{:S(2)}, u32[]{:S(2)}) collective-permute-start(bf16[2,64,512]{2,1,0:T(8,128)(2,1)S(1)} %add.36.stay_ref), channel_id=1, source_target_pairs={{0,16},{4,20},{8,24},{12,28},{16,0},{20,4},{24,8},{28,12},{1,17},{... | collective-permute-start | bytes 393224 | tf_op jit(solution)/shard_map/ppermute | solution.py:1112
  214.5 1.5 collective-permute-start.61
  215.9 1.7 collective-permute-start.55
  217.7 3.4 %collective-permute-start.57 = (bf16[2,64,512]{2,1,0:T(8,128)(2,1)S(1)}, bf16[2,64,512]{2,1,0:T(8,128)(2,1)S(1)}, u32[]{:S(2)}, u32[]{:S(2)}) collective-permute-start(bf16[2,64,512]{2,1,0:T(8,128)(2,1)S(1)} %add.37.own_ref), channel_id=1, source_target_pairs={{0,8},{4,12},{8,0},{12,4},{16,24},{20,28},{24,16},{28,20},{1,9},{5... | collective-permute-start | bytes 393224 | tf_op jit(solution)/shard_map/ppermute | solution.py:1112
  221.7 2.7 %collective-permute-done.55.arrived_ref = bf16[2,72,512]{2,1,0:T(8,128)(2,1)S(1)} collective-permute-done((bf16[2,72,512]{2,1,0:T(8,128)(2,1)S(1)}, bf16[2,72,512]{2,1,0:T(8,128)(2,1)S(1)}, u32[]{:S(2)}, u32[]{:S(2)}) %collective-permute-start.55) | collective-permute-done | bytes 147488 | tf_op jit(solution)/shard_map/ppermute | solution.py:1112
  224.4 1.2 collective-permute-start.59
  225.7 2.5 collective-permute-start.58
  228.9 1.7 collective-permute-start.62
  231.4 2.2 collective-permute-done.58.arrived_ref
  233.6 1.3 collective-permute-start.63
  235.0 1.3 collective-permute-done.60.other_ref
  237.7 1.9 collective-permute-start.64
  239.7 3.6 %collective-permute-start.66 = (bf16[2,64,512]{2,1,0:T(8,128)(2,1)S(1)}, bf16[2,64,512]{2,1,0:T(8,128)(2,1)S(1)}, u32[]{:S(2)}, u32[]{:S(2)}) collective-permute-start(bf16[2,64,512]{2,1,0:T(8,128)(2,1)S(1)} %add.42.own_ref), channel_id=1, source_target_pairs={{0,8},{4,12},{8,0},{12,4},{16,24},{20,28},{24,16},{28,20},{1,9},{5... | collective-permute-start | bytes 393224 | tf_op jit(solution)/shard_map/ppermute | solution.py:1112
  243.8 1.0 collective-permute-start.67
  244.9 1.2 collective-permute-done.65.refs_6_
  247.8 4.4 %feed_result.1 = (f32[2,512,512]{2,1,0:T(8,128)}, f32[2,512,512]{2,1,0:T(8,128)}) custom-call(s32[5]{0:T(128)} %stack.37.info_ref.refs_0_, bf16[4,128,512]{2,1,0:T(8,128)(2,1)} %copy-done, bf16[4,128,512]{2,1,0:T(8,128)(2,1)} %copy-done.31, bf16[4,64,512]{2,1,0:T(8,128)(2,1)} %copy-done.3, bf16[4,64,512]{2,1,0:T(8,128)(2,1)} %copy-done.33, ...), custom_call_target="tpu_custom_call" | custom-call | flops 1 | bytes 1 | tf_op jit(solution)/shard_map/feed_result/pallas_call | solution.py:985
  252.3 2.8 %collective-permute-done.68.refs_4_ = bf16[4,64,512]{2,1,0:T(8,128)(2,1)S(1)} collective-permute-done((bf16[4,64,512]{2,1,0:T(8,128)(2,1)S(1)}, bf16[4,64,512]{2,1,0:T(8,128)(2,1)S(1)}, u32[]{:S(2)}, u32[]{:S(2)}) %collective-permute-start.68) | collective-permute-done | bytes 262176 | tf_op jit(solution)/shard_map/ppermute | solution.py:1112
  255.8 3.3 %attn_result.1 = (f32[2,512,128]{2,1,0:T(8,128)}, f32[2,512,128]{2,1,0:T(8,128)}, f32[2,512,128]{2,1,0:T(8,128)}, f32[2,128,512]{2,1,0:T(8,128)}, f32[2,512]{1,0...) custom-call(s32[5]{0:T(128)} %stack.37.info_ref.refs_0_, ...), custom_call_target="tpu_custom_call" | custom-call | flops 1 | bytes 1 | tf_op jit(solution)/shard_map/attn_result/pallas_call | solution.py:985
  (226 shorter events, 35.3 us)
Async XLA Ops:
  2.5 8.8 %collective-permute-start = (bf16[512,512]{1,0:T(8,128)(2,1)}, bf16[512,512]{1,0:T(8,128)(2,1)S(1)}, u32[]{:S(2)}, u32[]{:S(2)}) collective-permute-start(bf16[512,512]{1,0:T(8,128)(2,1)} %pack_first.1.refs_4_.refs_9_.refs_26_.refs_6_), channel_id=1, source_target_pairs={{0,1},{1,0},{2,3},{3,2},{4,5},{5,4},{6,7},{7,6},{8,9},{9,8},{10,11... | collective-permute-start | bytes 1572872 | tf_op jit(solution)/shard_map/ppermute | solution.py:1112
  3.1 15.6 %collective-permute-start.1 = (bf16[512,512]{1,0:T(8,128)(2,1)}, bf16[512,512]{1,0:T(8,128)(2,1)S(1)}, u32[]{:S(2)}, u32[]{:S(2)}) collective-permute-start(bf16[512,512]{1,0:T(8,128)(2,1)} %pack_first.1.refs_4_.refs_9_.refs_26_.refs_6_), channel_id=1, source_target_pairs={{0,2},{1,3},{2,0},{3,1},{4,6},{5,7},{6,4},{7,5},{8,10},{9,11},{10,... | collective-permute-start | bytes 1572872 | tf_op jit(solution)/shard_map/ppermute | solution.py:1112
  11.2 19.1 %collective-permute-start.8 = (bf16[528,512]{1,0:T(8,128)(2,1)}, bf16[528,512]{1,0:T(8,128)(2,1)}, u32[]{:S(2)}, u32[]{:S(2)}) collective-permute-start(bf16[528,512]{1,0:T(8,128)(2,1)} %get-tuple-element.183), channel_id=1, source_target_pairs={{0,2},{1,3},{2,0},{3,1},{4,6},{5,7},{6,4},{7,5},{8,10},{9,11},{10,... | collective-permute-start | bytes 1622024 | tf_op jit(solution)/shard_map/ppermute | solution.py:1112
  11.3 34.6 %collective-permute-start.7 = (bf16[1056,512]{1,0:T(8,128)(2,1)}, bf16[1056,512]{1,0:T(8,128)(2,1)S(1)}, u32[]{:S(2)}, u32[]{:S(2)}) collective-permute-start(bf16[1056,512]{1,0:T(8,128)(2,1)} %get-tuple-element.202.refs_2_.refs_19_), channel_id=1, source_target_pairs={{0,1},{1,0},{2,3},{3,2},{4,5},{5,4},{6,7},{7,6},{8,9},{9,8},{10,11... | collective-permute-start | bytes 3244040 | tf_op jit(solution)/shard_map/ppermute | solution.py:1112
  25.0 9.9 %collective-permute-start.5 = (bf16[4,96,256]{2,1,0:T(8,128)(2,1)}, bf16[4,96,256]{2,1,0:T(8,128)(2,1)S(1)}, u32[]{:S(2)}, u32[]{:S(2)}) collective-permute-start(bf16[4,96,256]{2,1,0:T(8,128)(2,1)} %get-tuple-element.196), channel_id=1, source_target_pairs={{0,3},{1,2},{2,1},{3,0},{4,7},{5,6},{6,5},{7,4},{8,11},{9,10},{10,... | collective-permute-start | bytes 589832 | tf_op jit(solution)/shard_map/ppermute | solution.py:1112
  26.8 3.5 %collective-permute-start.4 = (bf16[4,80,256]{2,1,0:T(8,128)(2,1)}, bf16[4,80,256]{2,1,0:T(8,128)(2,1)S(1)}, u32[]{:S(2)}, u32[]{:S(2)}) collective-permute-start(bf16[4,80,256]{2,1,0:T(8,128)(2,1)} %get-tuple-element.195), channel_id=1, source_target_pairs={{0,1},{1,0},{2,3},{3,2},{4,5},{5,4},{6,7},{7,6},{8,9},{9,8},{10,11... | collective-permute-start | bytes 491528 | tf_op jit(solution)/shard_map/ppermute | solution.py:1112
  27.2 7.7 %collective-permute-start.6 = (bf16[4,16,256]{2,1,0:T(8,128)(2,1)}, bf16[4,16,256]{2,1,0:T(8,128)(2,1)S(1)}, u32[]{:S(2)}, u32[]{:S(2)}) collective-permute-start(bf16[4,16,256]{2,1,0:T(8,128)(2,1)} %get-tuple-element.191), channel_id=1, source_target_pairs={{0,2},{1,3},{2,0},{3,1},{4,6},{5,7},{6,4},{7,5},{8,10},{9,11},{10,... | collective-permute-start | bytes 98312 | tf_op jit(solution)/shard_map/ppermute | solution.py:1112
  30.3 14.3 %collective-permute-start.9 = (bf16[528,512]{1,0:T(8,128)(2,1)}, bf16[528,512]{1,0:T(8,128)(2,1)S(1)}, u32[]{:S(2)}, u32[]{:S(2)}) collective-permute-start(bf16[528,512]{1,0:T(8,128)(2,1)} %collective-permute-done.8.refs_3_.refs_21_), channel_id=1, source_target_pairs={{0,4},{4,0},{8,12},{12,8},{16,20},{20,16},{24,28},{28,24},{1,5},{5... | collective-permute-start | bytes 1622024 | tf_op jit(solution)/shard_map/ppermute | solution.py:1112
  34.9 16.6 %collective-permute-start.13 = (bf16[512,512]{1,0:T(8,128)(2,1)S(1)}, bf16[512,512]{1,0:T(8,128)(2,1)S(1)}, u32[]{:S(2)}, u32[]{:S(2)}) collective-permute-start(bf16[512,512]{1,0:T(8,128)(2,1)S(1)} %copy-done.19), channel_id=1, source_target_pairs={{0,2},{1,3},{2,0},{3,1},{4,6},{5,7},{6,4},{7,5},{8,10},{9,11},{10,... | collective-permute-start | bytes 1572872 | tf_op jit(solution)/shard_map/ppermute | solution.py:1112
  36.7 15.1 %collective-permute-start.10 = (bf16[528,512]{1,0:T(8,128)(2,1)}, bf16[528,512]{1,0:T(8,128)(2,1)}, u32[]{:S(2)}, u32[]{:S(2)}) collective-permute-start(bf16[528,512]{1,0:T(8,128)(2,1)} %collective-permute-done.8.refs_3_.refs_21_), channel_id=1, source_target_pairs={{0,1},{1,0},{2,3},{3,2},{4,5},{5,4},{6,7},{7,6},{8,9},{9,8},{10,11... | collective-permute-start | bytes 1622024 | tf_op jit(solution)/shard_map/ppermute | solution.py:1112
  44.6 7.2 %collective-permute-start.11 = (bf16[528,512]{1,0:T(8,128)(2,1)S(1)}, bf16[528,512]{1,0:T(8,128)(2,1)}, u32[]{:S(2)}, u32[]{:S(2)}) collective-permute-start(bf16[528,512]{1,0:T(8,128)(2,1)S(1)} %collective-permute-done.9.refs_4_.refs_22_), channel_id=1, source_target_pairs={{0,1},{1,0},{2,3},{3,2},{4,5},{5,4},{6,7},{7,6},{8,9},{9,8},{10,11... | collective-permute-start | bytes 1622024 | tf_op jit(solution)/shard_map/ppermute | solution.py:1112
  45.2 16.1 %collective-permute-start.19 = (bf16[528,512]{1,0:T(8,128)(2,1)}, bf16[528,512]{1,0:T(8,128)(2,1)}, u32[]{:S(2)}, u32[]{:S(2)}) collective-permute-start(bf16[528,512]{1,0:T(8,128)(2,1)} %get-tuple-element.225), channel_id=1, source_target_pairs={{0,2},{1,3},{2,0},{3,1},{4,6},{5,7},{6,4},{7,5},{8,10},{9,11},{10,... | collective-permute-start | bytes 1622024 | tf_op jit(solution)/shard_map/ppermute | solution.py:1112
  45.9 5.9 %collective-permute-start.12 = (bf16[512,512]{1,0:T(8,128)(2,1)S(1)}, bf16[512,512]{1,0:T(8,128)(2,1)S(1)}, u32[]{:S(2)}, u32[]{:S(2)}) collective-permute-start(bf16[512,512]{1,0:T(8,128)(2,1)S(1)} %copy-done.19), channel_id=1, source_target_pairs={{0,1},{1,0},{2,3},{3,2},{4,5},{5,4},{6,7},{7,6},{8,9},{9,8},{10,11... | collective-permute-start | bytes 1572872 | tf_op jit(solution)/shard_map/ppermute | solution.py:1112
  61.3 18.1 %collective-permute-start.20 = (bf16[528,512]{1,0:T(8,128)(2,1)}, bf16[528,512]{1,0:T(8,128)(2,1)S(1)}, u32[]{:S(2)}, u32[]{:S(2)}) collective-permute-start(bf16[528,512]{1,0:T(8,128)(2,1)} %collective-permute-done.19.refs_5_), channel_id=1, source_target_pairs={{0,4},{4,0},{8,12},{12,8},{16,20},{20,16},{24,28},{28,24},{1,5},{5... | collective-permute-start | bytes 1622024 | tf_op jit(solution)/shard_map/ppermute | solution.py:1112
  62.8 17.2 %collective-permute-start.18 = (bf16[1056,512]{1,0:T(8,128)(2,1)}, bf16[1056,512]{1,0:T(8,128)(2,1)S(1)}, u32[]{:S(2)}, u32[]{:S(2)}) collective-permute-start(bf16[1056,512]{1,0:T(8,128)(2,1)} %get-tuple-element.223.refs_3_), channel_id=1, source_target_pairs={{0,1},{1,0},{2,3},{3,2},{4,5},{5,4},{6,7},{7,6},{8,9},{9,8},{10,11... | collective-permute-start | bytes 3244040 | tf_op jit(solution)/shard_map/ppermute | solution.py:1112
  62.8 8.1 %collective-permute-start.16 = (bf16[4,96,256]{2,1,0:T(8,128)(2,1)}, bf16[4,96,256]{2,1,0:T(8,128)(2,1)S(1)}, u32[]{:S(2)}, u32[]{:S(2)}) collective-permute-start(bf16[4,96,256]{2,1,0:T(8,128)(2,1)} %get-tuple-element.216), channel_id=1, source_target_pairs={{0,3},{1,2},{2,1},{3,0},{4,7},{5,6},{6,5},{7,4},{8,11},{9,10},{10,... | collective-permute-start | bytes 589832 | tf_op jit(solution)/shard_map/ppermute | solution.py:1112
  64.3 6.7 %collective-permute-start.15 = (bf16[4,80,256]{2,1,0:T(8,128)(2,1)}, bf16[4,80,256]{2,1,0:T(8,128)(2,1)S(1)}, u32[]{:S(2)}, u32[]{:S(2)}) collective-permute-start(bf16[4,80,256]{2,1,0:T(8,128)(2,1)} %get-tuple-element.215), channel_id=1, source_target_pairs={{0,1},{1,0},{2,3},{3,2},{4,5},{5,4},{6,7},{7,6},{8,9},{9,8},{10,11... | collective-permute-start | bytes 491528 | tf_op jit(solution)/shard_map/ppermute | solution.py:1112
  64.3 6.7 %collective-permute-start.17 = (bf16[4,16,256]{2,1,0:T(8,128)(2,1)}, bf16[4,16,256]{2,1,0:T(8,128)(2,1)S(1)}, u32[]{:S(2)}, u32[]{:S(2)}) collective-permute-start(bf16[4,16,256]{2,1,0:T(8,128)(2,1)} %get-tuple-element.212), channel_id=1, source_target_pairs={{0,2},{1,3},{2,0},{3,1},{4,6},{5,7},{6,4},{7,5},{8,10},{9,11},{10,... | collective-permute-start | bytes 98312 | tf_op jit(solution)/shard_map/ppermute | solution.py:1112
  70.9 9.1 %collective-permute-start.21 = (bf16[528,512]{1,0:T(8,128)(2,1)}, bf16[528,512]{1,0:T(8,128)(2,1)S(1)}, u32[]{:S(2)}, u32[]{:S(2)}) collective-permute-start(bf16[528,512]{1,0:T(8,128)(2,1)} %collective-permute-done.19.refs_5_), channel_id=1, source_target_pairs={{0,1},{1,0},{2,3},{3,2},{4,5},{5,4},{6,7},{7,6},{8,9},{9,8},{10,11... | collective-permute-start | bytes 1622024 | tf_op jit(solution)/shard_map/ppermute | solution.py:1112
  104.3 8.1 %collective-permute-start.25 = (bf16[4,96,256]{2,1,0:T(8,128)(2,1)}, bf16[4,96,256]{2,1,0:T(8,128)(2,1)S(1)}, u32[]{:S(2)}, u32[]{:S(2)}) collective-permute-start(bf16[4,96,256]{2,1,0:T(8,128)(2,1)} %get-tuple-element.240), channel_id=1, source_target_pairs={{0,3},{1,2},{2,1},{3,0},{4,7},{5,6},{6,5},{7,4},{8,11},{9,10},{10,... | collective-permute-start | bytes 589832 | tf_op jit(solution)/shard_map/ppermute | solution.py:1112
  105.3 7.1 %collective-permute-start.24 = (bf16[4,80,256]{2,1,0:T(8,128)(2,1)}, bf16[4,80,256]{2,1,0:T(8,128)(2,1)S(1)}, u32[]{:S(2)}, u32[]{:S(2)}) collective-permute-start(bf16[4,80,256]{2,1,0:T(8,128)(2,1)} %get-tuple-element.239), channel_id=1, source_target_pairs={{0,1},{1,0},{2,3},{3,2},{4,5},{5,4},{6,7},{7,6},{8,9},{9,8},{10,11... | collective-permute-start | bytes 491528 | tf_op jit(solution)/shard_map/ppermute | solution.py:1112
  105.7 6.7 %collective-permute-start.26 = (bf16[4,16,256]{2,1,0:T(8,128)(2,1)}, bf16[4,16,256]{2,1,0:T(8,128)(2,1)S(1)}, u32[]{:S(2)}, u32[]{:S(2)}) collective-permute-start(bf16[4,16,256]{2,1,0:T(8,128)(2,1)} %get-tuple-element.234), channel_id=1, source_target_pairs={{0,2},{1,3},{2,0},{3,1},{4,6},{5,7},{6,4},{7,5},{8,10},{9,11},{10,... | collective-permute-start | bytes 98312 | tf_op jit(solution)/shard_map/ppermute | solution.py:1112
  112.4 24.9 %collective-permute-start.28 = (bf16[8,128,512]{2,1,0:T(8,128)(2,1)S(1)}, bf16[8,128,512]{2,1,0:T(8,128)(2,1)S(1)}, u32[]{:S(2)}, u32[]{:S(2)}) collective-permute-start(bf16[8,128,512]{2,1,0:T(8,128)(2,1)S(1)} %core_sum.5), channel_id=1, source_target_pairs={{0,2},{1,3},{2,0},{3,1},{4,6},{5,7},{6,4},{7,5},{8,10},{9,11},{10,... | collective-permute-start | bytes 3145736 | tf_op jit(solution)/shard_map/ppermute | solution.py:1112
  113.8 25.1 %collective-permute-start.27 = (bf16[8,128,512]{2,1,0:T(8,128)(2,1)}, bf16[8,128,512]{2,1,0:T(8,128)(2,1)}, u32[]{:S(2)}, u32[]{:S(2)}) collective-permute-start(bf16[8,128,512]{2,1,0:T(8,128)(2,1)} %get-tuple-element.255), channel_id=1, source_target_pairs={{0,1},{1,0},{2,3},{3,2},{4,5},{5,4},{6,7},{7,6},{8,9},{9,8},{10,11... | collective-permute-start | bytes 3145736 | tf_op jit(solution)/shard_map/ppermute | solution.py:1112
  136.1 6.5 %collective-permute-start.29 = (bf16[8,64,512]{2,1,0:T(8,128)(2,1)}, bf16[8,64,512]{2,1,0:T(8,128)(2,1)}, u32[]{:S(2)}, u32[]{:S(2)}) collective-permute-start(bf16[8,64,512]{2,1,0:T(8,128)(2,1)} %get-tuple-element.259), channel_id=1, source_target_pairs={{0,1},{1,0},{2,3},{3,2},{4,5},{5,4},{6,7},{7,6},{8,9},{9,8},{10,11... | collective-permute-start | bytes 1572872 | tf_op jit(solution)/shard_map/ppermute | solution.py:1112
  137.3 9.2 %collective-permute-start.30 = (bf16[4,80,256]{2,1,0:T(8,128)(2,1)}, bf16[4,80,256]{2,1,0:T(8,128)(2,1)S(1)}, u32[]{:S(2)}, u32[]{:S(2)}) collective-permute-start(bf16[4,80,256]{2,1,0:T(8,128)(2,1)} %get-tuple-element.263), channel_id=1, source_target_pairs={{0,1},{1,0},{2,3},{3,2},{4,5},{5,4},{6,7},{7,6},{8,9},{9,8},{10,11... | collective-permute-start | bytes 491528 | tf_op jit(solution)/shard_map/ppermute | solution.py:1112
  137.3 9.2 %collective-permute-start.31 = (bf16[4,96,256]{2,1,0:T(8,128)(2,1)}, bf16[4,96,256]{2,1,0:T(8,128)(2,1)S(1)}, u32[]{:S(2)}, u32[]{:S(2)}) collective-permute-start(bf16[4,96,256]{2,1,0:T(8,128)(2,1)} %get-tuple-element.265), channel_id=1, source_target_pairs={{0,3},{1,2},{2,1},{3,0},{4,7},{5,6},{6,5},{7,4},{8,11},{9,10},{10,... | collective-permute-start | bytes 589832 | tf_op jit(solution)/shard_map/ppermute | solution.py:1112
  138.8 15.6 %collective-permute-start.33 = (bf16[8,64,512]{2,1,0:T(8,128)(2,1)}, bf16[8,64,512]{2,1,0:T(8,128)(2,1)S(1)}, u32[]{:S(2)}, u32[]{:S(2)}) collective-permute-start(bf16[8,64,512]{2,1,0:T(8,128)(2,1)} %get-tuple-element.278), channel_id=1, source_target_pairs={{0,1},{1,0},{2,3},{3,2},{4,5},{5,4},{6,7},{7,6},{8,9},{9,8},{10,11... | collective-permute-start | bytes 1572872 | tf_op jit(solution)/shard_map/ppermute | solution.py:1112
  142.1 14.5 %collective-permute-start.34 = (bf16[4,128,512]{2,1,0:T(8,128)(2,1)}, bf16[4,128,512]{2,1,0:T(8,128)(2,1)S(1)}, u32[]{:S(2)}, u32[]{:S(2)}) collective-permute-start(bf16[4,128,512]{2,1,0:T(8,128)(2,1)} %get-tuple-element.257), channel_id=1, source_target_pairs={{0,4},{4,0},{8,12},{12,8},{16,20},{20,16},{24,28},{28,24},{1,5},{5... | collective-permute-start | bytes 1572872 | tf_op jit(solution)/shard_map/ppermute | solution.py:1112
  142.6 3.9 %collective-permute-start.32 = (bf16[4,16,256]{2,1,0:T(8,128)(2,1)S(1)}, bf16[4,16,256]{2,1,0:T(8,128)(2,1)S(1)}, u32[]{:S(2)}, u32[]{:S(2)}) collective-permute-start(bf16[4,16,256]{2,1,0:T(8,128)(2,1)S(1)} %copy-done.52), channel_id=1, source_target_pairs={{0,2},{1,3},{2,0},{3,1},{4,6},{5,7},{6,4},{7,5},{8,10},{9,11},{10,... | collective-permute-start | bytes 98312 | tf_op jit(solution)/shard_map/ppermute | solution.py:1112
  146.5 12.4 %collective-permute-start.35 = (bf16[8,64,512]{2,1,0:T(8,128)(2,1)}, bf16[8,64,512]{2,1,0:T(8,128)(2,1)S(1)}, u32[]{:S(2)}, u32[]{:S(2)}) collective-permute-start(bf16[8,64,512]{2,1,0:T(8,128)(2,1)} %get-tuple-element.286), channel_id=1, source_target_pairs={{0,1},{1,0},{2,3},{3,2},{4,5},{5,4},{6,7},{7,6},{8,9},{9,8},{10,11... | collective-permute-start | bytes 1572872 | tf_op jit(solution)/shard_map/ppermute | solution.py:1112
  146.6 14.4 %collective-permute-start.36 = (bf16[8,64,512]{2,1,0:T(8,128)(2,1)S(1)}, bf16[8,64,512]{2,1,0:T(8,128)(2,1)S(1)}, u32[]{:S(2)}, u32[]{:S(2)}) collective-permute-start(bf16[8,64,512]{2,1,0:T(8,128)(2,1)S(1)} %core_sum.6), channel_id=1, source_target_pairs={{0,2},{1,3},{2,0},{3,1},{4,6},{5,7},{6,4},{7,5},{8,10},{9,11},{10,... | collective-permute-start | bytes 1572872 | tf_op jit(solution)/shard_map/ppermute | solution.py:1112
  153.9 12.1 %collective-permute-start.37 = (bf16[8,72,512]{2,1,0:T(8,128)(2,1)}, bf16[8,72,512]{2,1,0:T(8,128)(2,1)S(1)}, u32[]{:S(2)}, u32[]{:S(2)}) collective-permute-start(bf16[8,72,512]{2,1,0:T(8,128)(2,1)} %get-tuple-element.290), channel_id=1, source_target_pairs={{0,1},{1,0},{2,3},{3,2},{4,5},{5,4},{6,7},{7,6},{8,9},{9,8},{10,11... | collective-permute-start | bytes 1769480 | tf_op jit(solution)/shard_map/ppermute | solution.py:1112
  157.3 8.0 %collective-permute-start.38 = (bf16[2,128,512]{2,1,0:T(8,128)(2,1)S(1)}, bf16[2,128,512]{2,1,0:T(8,128)(2,1)S(1)}, u32[]{:S(2)}, u32[]{:S(2)}) collective-permute-start(bf16[2,128,512]{2,1,0:T(8,128)(2,1)S(1)} %get-tuple-element.283), channel_id=1, source_target_pairs={{0,8},{4,12},{8,0},{12,4},{16,24},{20,28},{24,16},{28,20},{1,9},{5... | collective-permute-start | bytes 786440 | tf_op jit(solution)/shard_map/ppermute | solution.py:1112
  161.7 8.0 %collective-permute-start.39 = (bf16[4,64,512]{2,1,0:T(8,128)(2,1)S(1)}, bf16[4,64,512]{2,1,0:T(8,128)(2,1)S(1)}, u32[]{:S(2)}, u32[]{:S(2)}) collective-permute-start(bf16[4,64,512]{2,1,0:T(8,128)(2,1)S(1)} %get-tuple-element.288), channel_id=1, source_target_pairs={{0,4},{4,0},{8,12},{12,8},{16,20},{20,16},{24,28},{28,24},{1,5},{5... | collective-permute-start | bytes 786440 | tf_op jit(solution)/shard_map/ppermute | solution.py:1112
  163.3 19.5 %collective-permute-start.43 = (bf16[8,72,512]{2,1,0:T(8,128)(2,1)S(1)}, bf16[8,72,512]{2,1,0:T(8,128)(2,1)S(1)}, u32[]{:S(2)}, u32[]{:S(2)}) collective-permute-start(bf16[8,72,512]{2,1,0:T(8,128)(2,1)S(1)} %copy-done.48), channel_id=1, source_target_pairs={{0,1},{1,0},{2,3},{3,2},{4,5},{5,4},{6,7},{7,6},{8,9},{9,8},{10,11... | collective-permute-start | bytes 1769480 | tf_op jit(solution)/shard_map/ppermute | solution.py:1112
  163.3 7.8 %collective-permute-start.40 = (bf16[8,64,512]{2,1,0:T(8,128)(2,1)S(1)}, bf16[8,64,512]{2,1,0:T(8,128)(2,1)S(1)}, u32[]{:S(2)}, u32[]{:S(2)}) collective-permute-start(bf16[8,64,512]{2,1,0:T(8,128)(2,1)S(1)} %copy-done.51), channel_id=1, source_target_pairs={{0,1},{1,0},{2,3},{3,2},{4,5},{5,4},{6,7},{7,6},{8,9},{9,8},{10,11... | collective-permute-start | bytes 1572872 | tf_op jit(solution)/shard_map/ppermute | solution.py:1112
  165.2 14.9 %collective-permute-start.41 = (bf16[8,64,512]{2,1,0:T(8,128)(2,1)S(1)}, bf16[8,64,512]{2,1,0:T(8,128)(2,1)S(1)}, u32[]{:S(2)}, u32[]{:S(2)}) collective-permute-start(bf16[8,64,512]{2,1,0:T(8,128)(2,1)S(1)} %core_sum.7), channel_id=1, source_target_pairs={{0,2},{1,3},{2,0},{3,1},{4,6},{5,7},{6,4},{7,5},{8,10},{9,11},{10,... | collective-permute-start | bytes 1572872 | tf_op jit(solution)/shard_map/ppermute | solution.py:1112
  166.0 15.5 %collective-permute-start.42 = (bf16[8,64,512]{2,1,0:T(8,128)(2,1)S(1)}, bf16[8,64,512]{2,1,0:T(8,128)(2,1)S(1)}, u32[]{:S(2)}, u32[]{:S(2)}) collective-permute-start(bf16[8,64,512]{2,1,0:T(8,128)(2,1)S(1)} %copy-done.50), channel_id=1, source_target_pairs={{0,1},{1,0},{2,3},{3,2},{4,5},{5,4},{6,7},{7,6},{8,9},{9,8},{10,11... | collective-permute-start | bytes 1572872 | tf_op jit(solution)/shard_map/ppermute | solution.py:1112
  169.7 23.0 %collective-permute-start.44 = (bf16[8,72,512]{2,1,0:T(8,128)(2,1)S(1)}, bf16[8,72,512]{2,1,0:T(8,128)(2,1)S(1)}, u32[]{:S(2)}, u32[]{:S(2)}) collective-permute-start(bf16[8,72,512]{2,1,0:T(8,128)(2,1)S(1)} %core_sum.8), channel_id=1, source_target_pairs={{0,2},{1,3},{2,0},{3,1},{4,6},{5,7},{6,4},{7,5},{8,10},{9,11},{10,... | collective-permute-start | bytes 1769480 | tf_op jit(solution)/shard_map/ppermute | solution.py:1112
  180.8 14.3 %collective-permute-start.45 = (bf16[4,64,512]{2,1,0:T(8,128)(2,1)S(1)}, bf16[4,64,512]{2,1,0:T(8,128)(2,1)S(1)}, u32[]{:S(2)}, u32[]{:S(2)}) collective-permute-start(bf16[4,64,512]{2,1,0:T(8,128)(2,1)S(1)} %get-tuple-element.299), channel_id=1, source_target_pairs={{0,4},{4,0},{8,12},{12,8},{16,20},{20,16},{24,28},{28,24},{1,5},{5... | collective-permute-start | bytes 786440 | tf_op jit(solution)/shard_map/ppermute | solution.py:1112
  181.5 26.8 %collective-permute-start.49 = (bf16[8,64,512]{2,1,0:T(8,128)(2,1)S(1)}, bf16[8,64,512]{2,1,0:T(8,128)(2,1)S(1)}, u32[]{:S(2)}, u32[]{:S(2)}) collective-permute-start(bf16[8,64,512]{2,1,0:T(8,128)(2,1)S(1)} %copy-done.49), channel_id=1, source_target_pairs={{0,1},{1,0},{2,3},{3,2},{4,5},{5,4},{6,7},{7,6},{8,9},{9,8},{10,11... | collective-permute-start | bytes 1572872 | tf_op jit(solution)/shard_map/ppermute | solution.py:1112
  181.6 26.7 %collective-permute-start.50 = (bf16[8,64,512]{2,1,0:T(8,128)(2,1)S(1)}, bf16[8,64,512]{2,1,0:T(8,128)(2,1)S(1)}, u32[]{:S(2)}, u32[]{:S(2)}) collective-permute-start(bf16[8,64,512]{2,1,0:T(8,128)(2,1)S(1)} %core_sum.9), channel_id=1, source_target_pairs={{0,2},{1,3},{2,0},{3,1},{4,6},{5,7},{6,4},{7,5},{8,10},{9,11},{10,... | collective-permute-start | bytes 1572872 | tf_op jit(solution)/shard_map/ppermute | solution.py:1112
  182.8 16.4 %collective-permute-start.47 = (bf16[2,128,512]{2,1,0:T(8,128)(2,1)S(1)}, bf16[2,128,512]{2,1,0:T(8,128)(2,1)S(1)}, u32[]{:S(2)}, u32[]{:S(2)}) collective-permute-start(bf16[2,128,512]{2,1,0:T(8,128)(2,1)S(1)} %add.33.stay_ref), channel_id=1, source_target_pairs={{0,16},{4,20},{8,24},{12,28},{16,0},{20,4},{24,8},{28,12},{1,17},{... | collective-permute-start | bytes 786440 | tf_op jit(solution)/shard_map/ppermute | solution.py:1112
  192.7 6.4 %collective-permute-start.46 = (bf16[2,64,512]{2,1,0:T(8,128)(2,1)S(1)}, bf16[2,64,512]{2,1,0:T(8,128)(2,1)S(1)}, u32[]{:S(2)}, u32[]{:S(2)}) collective-permute-start(bf16[2,64,512]{2,1,0:T(8,128)(2,1)S(1)} %get-tuple-element.294), channel_id=1, source_target_pairs={{0,8},{4,12},{8,0},{12,4},{16,24},{20,28},{24,16},{28,20},{1,9},{5... | collective-permute-start | bytes 393224 | tf_op jit(solution)/shard_map/ppermute | solution.py:1112
  195.1 18.1 %collective-permute-start.51 = (bf16[4,72,512]{2,1,0:T(8,128)(2,1)S(1)}, bf16[4,72,512]{2,1,0:T(8,128)(2,1)S(1)}, u32[]{:S(2)}, u32[]{:S(2)}) collective-permute-start(bf16[4,72,512]{2,1,0:T(8,128)(2,1)S(1)} %get-tuple-element.305), channel_id=1, source_target_pairs={{0,4},{4,0},{8,12},{12,8},{16,20},{20,16},{24,28},{28,24},{1,5},{5... | collective-permute-start | bytes 884744 | tf_op jit(solution)/shard_map/ppermute | solution.py:1112
  199.3 14.6 %collective-permute-start.52 = (bf16[2,128,512]{2,1,0:T(8,128)(2,1)S(1)}, bf16[2,128,512]{2,1,0:T(8,128)(2,1)S(1)}, u32[]{:S(2)}, u32[]{:S(2)}) collective-permute-start(bf16[2,128,512]{2,1,0:T(8,128)(2,1)S(1)} %add.35.own_ref), channel_id=1, source_target_pairs={{0,8},{4,12},{8,0},{12,4},{16,24},{20,28},{24,16},{28,20},{1,9},{5... | collective-permute-start | bytes 786440 | tf_op jit(solution)/shard_map/ppermute | solution.py:1112
  199.5 8.8 %collective-permute-start.48 = (bf16[2,64,512]{2,1,0:T(8,128)(2,1)S(1)}, bf16[2,64,512]{2,1,0:T(8,128)(2,1)S(1)}, u32[]{:S(2)}, u32[]{:S(2)}) collective-permute-start(bf16[2,64,512]{2,1,0:T(8,128)(2,1)S(1)} %get-tuple-element.310), channel_id=1, source_target_pairs={{0,8},{4,12},{8,0},{12,4},{16,24},{20,28},{24,16},{28,20},{1,9},{5... | collective-permute-start | bytes 393224 | tf_op jit(solution)/shard_map/ppermute | solution.py:1112
  209.1 12.0 %collective-permute-start.54 = (bf16[4,64,512]{2,1,0:T(8,128)(2,1)S(1)}, bf16[4,64,512]{2,1,0:T(8,128)(2,1)S(1)}, u32[]{:S(2)}, u32[]{:S(2)}) collective-permute-start(bf16[4,64,512]{2,1,0:T(8,128)(2,1)S(1)} %get-tuple-element.318), channel_id=1, source_target_pairs={{0,4},{4,0},{8,12},{12,8},{16,20},{20,16},{24,28},{28,24},{1,5},{5... | collective-permute-start | bytes 786440 | tf_op jit(solution)/shard_map/ppermute | solution.py:1112
  210.2 7.5 %collective-permute-start.53 = (bf16[2,64,512]{2,1,0:T(8,128)(2,1)S(1)}, bf16[2,64,512]{2,1,0:T(8,128)(2,1)S(1)}, u32[]{:S(2)}, u32[]{:S(2)}) collective-permute-start(bf16[2,64,512]{2,1,0:T(8,128)(2,1)S(1)} %add.36.stay_ref), channel_id=1, source_target_pairs={{0,16},{4,20},{8,24},{12,28},{16,0},{20,4},{24,8},{28,12},{1,17},{... | collective-permute-start | bytes 393224 | tf_op jit(solution)/shard_map/ppermute | solution.py:1112
  214.5 25.1 %collective-permute-start.61 = (bf16[4,128,512]{2,1,0:T(8,128)(2,1)S(1)}, bf16[4,128,512]{2,1,0:T(8,128)(2,1)S(1)}, u32[]{:S(2)}, u32[]{:S(2)}) collective-permute-start(bf16[4,128,512]{2,1,0:T(8,128)(2,1)S(1)} %join.5.refs_1_), channel_id=1, source_target_pairs={{0,4},{4,0},{8,12},{12,8},{16,20},{20,16},{24,28},{28,24},{1,5},{5... | collective-permute-start | bytes 1572872 | tf_op jit(solution)/shard_map/ppermute | solution.py:1112
  215.9 8.5 %collective-permute-start.55 = (bf16[2,72,512]{2,1,0:T(8,128)(2,1)S(1)}, bf16[2,72,512]{2,1,0:T(8,128)(2,1)S(1)}, u32[]{:S(2)}, u32[]{:S(2)}) collective-permute-start(bf16[2,72,512]{2,1,0:T(8,128)(2,1)S(1)} %get-tuple-element.321), channel_id=1, source_target_pairs={{0,8},{4,12},{8,0},{12,4},{16,24},{20,28},{24,16},{28,20},{1,9},{5... | collective-permute-start | bytes 442376 | tf_op jit(solution)/shard_map/ppermute | solution.py:1112
  217.7 10.5 %collective-permute-start.56 = (bf16[2,64,512]{2,1,0:T(8,128)(2,1)S(1)}, bf16[2,64,512]{2,1,0:T(8,128)(2,1)S(1)}, u32[]{:S(2)}, u32[]{:S(2)}) collective-permute-start(bf16[2,64,512]{2,1,0:T(8,128)(2,1)S(1)} %add.34.stay_ref), channel_id=1, source_target_pairs={{0,16},{4,20},{8,24},{12,28},{16,0},{20,4},{24,8},{28,12},{1,17},{... | collective-permute-start | bytes 393224 | tf_op jit(solution)/shard_map/ppermute | solution.py:1112
  217.7 10.6 %collective-permute-start.57 = (bf16[2,64,512]{2,1,0:T(8,128)(2,1)S(1)}, bf16[2,64,512]{2,1,0:T(8,128)(2,1)S(1)}, u32[]{:S(2)}, u32[]{:S(2)}) collective-permute-start(bf16[2,64,512]{2,1,0:T(8,128)(2,1)S(1)} %add.37.own_ref), channel_id=1, source_target_pairs={{0,8},{4,12},{8,0},{12,4},{16,24},{20,28},{24,16},{28,20},{1,9},{5... | collective-permute-start | bytes 393224 | tf_op jit(solution)/shard_map/ppermute | solution.py:1112
  224.4 10.5 %collective-permute-start.59 = (bf16[2,72,512]{2,1,0:T(8,128)(2,1)S(1)}, bf16[2,72,512]{2,1,0:T(8,128)(2,1)S(1)}, u32[]{:S(2)}, u32[]{:S(2)}) collective-permute-start(bf16[2,72,512]{2,1,0:T(8,128)(2,1)S(1)} %add.38.stay_ref), channel_id=1, source_target_pairs={{0,16},{4,20},{8,24},{12,28},{16,0},{20,4},{24,8},{28,12},{1,17},{... | collective-permute-start | bytes 442376 | tf_op jit(solution)/shard_map/ppermute | solution.py:1112
  225.7 7.9 %collective-permute-start.58 = (bf16[2,64,512]{2,1,0:T(8,128)(2,1)S(1)}, bf16[2,64,512]{2,1,0:T(8,128)(2,1)S(1)}, u32[]{:S(2)}, u32[]{:S(2)}) collective-permute-start(bf16[2,64,512]{2,1,0:T(8,128)(2,1)S(1)} %get-tuple-element.328), channel_id=1, source_target_pairs={{0,8},{4,12},{8,0},{12,4},{16,24},{20,28},{24,16},{28,20},{1,9},{5... | collective-permute-start | bytes 393224 | tf_op jit(solution)/shard_map/ppermute | solution.py:1112
  228.9 10.6 %collective-permute-start.62 = (bf16[4,64,512]{2,1,0:T(8,128)(2,1)S(1)}, bf16[4,64,512]{2,1,0:T(8,128)(2,1)S(1)}, u32[]{:S(2)}, u32[]{:S(2)}) collective-permute-start(bf16[4,64,512]{2,1,0:T(8,128)(2,1)S(1)} %join.6.refs_3_), channel_id=1, source_target_pairs={{0,4},{4,0},{8,12},{12,8},{16,20},{20,16},{24,28},{28,24},{1,5},{5... | collective-permute-start | bytes 786440 | tf_op jit(solution)/shard_map/ppermute | solution.py:1112
  230.6 5.7 %collective-permute-start.60 = (bf16[2,64,512]{2,1,0:T(8,128)(2,1)S(1)}, bf16[2,64,512]{2,1,0:T(8,128)(2,1)S(1)}, u32[]{:S(2)}, u32[]{:S(2)}) collective-permute-start(bf16[2,64,512]{2,1,0:T(8,128)(2,1)S(1)} %add.39.own_ref), channel_id=1, source_target_pairs={{0,8},{4,12},{8,0},{12,4},{16,24},{20,28},{24,16},{28,20},{1,9},{5... | collective-permute-start | bytes 393224 | tf_op jit(solution)/shard_map/ppermute | solution.py:1112
  233.6 6.0 %collective-permute-start.63 = (bf16[2,64,512]{2,1,0:T(8,128)(2,1)S(1)}, bf16[2,64,512]{2,1,0:T(8,128)(2,1)S(1)}, u32[]{:S(2)}, u32[]{:S(2)}) collective-permute-start(bf16[2,64,512]{2,1,0:T(8,128)(2,1)S(1)} %add.40.stay_ref), channel_id=1, source_target_pairs={{0,16},{4,20},{8,24},{12,28},{16,0},{20,4},{24,8},{28,12},{1,17},{... | collective-permute-start | bytes 393224 | tf_op jit(solution)/shard_map/ppermute | solution.py:1112
  236.8 9.2 %collective-permute-start.65 = (bf16[4,64,512]{2,1,0:T(8,128)(2,1)S(1)}, bf16[4,64,512]{2,1,0:T(8,128)(2,1)S(1)}, u32[]{:S(2)}, u32[]{:S(2)}) collective-permute-start(bf16[4,64,512]{2,1,0:T(8,128)(2,1)S(1)} %join.7.refs_5_), channel_id=1, source_target_pairs={{0,4},{4,0},{8,12},{12,8},{16,20},{20,16},{24,28},{28,24},{1,5},{5... | collective-permute-start | bytes 786440 | tf_op jit(solution)/shard_map/ppermute | solution.py:1112
  237.7 5.6 %collective-permute-start.64 = (bf16[2,72,512]{2,1,0:T(8,128)(2,1)S(1)}, bf16[2,72,512]{2,1,0:T(8,128)(2,1)S(1)}, u32[]{:S(2)}, u32[]{:S(2)}) collective-permute-start(bf16[2,72,512]{2,1,0:T(8,128)(2,1)S(1)} %add.41.own_ref), channel_id=1, source_target_pairs={{0,8},{4,12},{8,0},{12,4},{16,24},{20,28},{24,16},{28,20},{1,9},{5... | collective-permute-start | bytes 442376 | tf_op jit(solution)/shard_map/ppermute | solution.py:1112
  239.7 6.5 %collective-permute-start.66 = (bf16[2,64,512]{2,1,0:T(8,128)(2,1)S(1)}, bf16[2,64,512]{2,1,0:T(8,128)(2,1)S(1)}, u32[]{:S(2)}, u32[]{:S(2)}) collective-permute-start(bf16[2,64,512]{2,1,0:T(8,128)(2,1)S(1)} %add.42.own_ref), channel_id=1, source_target_pairs={{0,8},{4,12},{8,0},{12,4},{16,24},{20,28},{24,16},{28,20},{1,9},{5... | collective-permute-start | bytes 393224 | tf_op jit(solution)/shard_map/ppermute | solution.py:1112
  243.8 8.4 %collective-permute-start.67 = (bf16[4,72,512]{2,1,0:T(8,128)(2,1)S(1)}, bf16[4,72,512]{2,1,0:T(8,128)(2,1)S(1)}, u32[]{:S(2)}, u32[]{:S(2)}) collective-permute-start(bf16[4,72,512]{2,1,0:T(8,128)(2,1)S(1)} %join.8.refs_1_), channel_id=1, source_target_pairs={{0,4},{4,0},{8,12},{12,8},{16,20},{20,16},{24,28},{28,24},{1,5},{5... | collective-permute-start | bytes 884744 | tf_op jit(solution)/shard_map/ppermute | solution.py:1112
  246.8 8.3 %collective-permute-start.68 = (bf16[4,64,512]{2,1,0:T(8,128)(2,1)S(1)}, bf16[4,64,512]{2,1,0:T(8,128)(2,1)S(1)}, u32[]{:S(2)}, u32[]{:S(2)}) collective-permute-start(bf16[4,64,512]{2,1,0:T(8,128)(2,1)S(1)} %join.9.refs_3_), channel_id=1, source_target_pairs={{0,4},{4,0},{8,12},{12,8},{16,20},{20,16},{24,28},{28,24},{1,5},{5... | collective-permute-start | bytes 786440 | tf_op jit(solution)/shard_map/ppermute | solution.py:1112
  (58 other events, 320.0 us)
where the time goes:
time: 260 us; the launch traced here: 259 us
  Pallas kernels  112 us (43%)
  waiting for transfers between devices  72.1 us (28%)
  starting transfers between devices  64.9 us (25%)
  local copies, waits for them, and re-layouts  7.87 us (3%)
    pallas_call x11, Pallas kernels, staged(): pl.pallas_call(kernel, out_shape=tuple(out), in_specs=[pl.BlockSpec(memor...  92.4 us
    ppermute x69, waiting for transfers between devices, swap(): return lax.ppermute(value, axis, [(i, i ^ bit) for i in range(size)])  72.1 us
    ppermute x69, starting transfers between devices, swap(): return lax.ppermute(value, axis, [(i, i ^ bit) for i in range(size)])  64.9 us
    pallas_call x30, Pallas kernels, call(): pl.pallas_call(body, out_shape=tuple(out), in_specs=in_specs, out_specs=t...  13.5 us
    unnamed x106, local copies, waits for them, and re-layouts  7.21 us
  transfers between devices with their start and end apart: 69, of which 29 were waited for; matrix products, arithmetic and copies ran while one was open for 0% of the time, Pallas kernels for 33%

commit v1 on v0

--- a/solution.py
+++ b/solution.py
@@ -1396,18 +1396,19 @@
     )
     a1 = Flow(index, a1, core_swap(a1))
     for flow in (
-        f1, f2, g1, a1, f2, g1, f1, a2, a1, f1, g1, f2,
-        f1, a2, a1, f2, f1, a2, a1, g1, f1, a2, a1, g1,
-        f2, f1, a2, a1, g1,
+        f1, f2, g1, a1, f1, f2, g1, a2, a1, f1, g1, f2,
+        a2, a1, f1, f2, a1, f1, a2, g1, f1, a1, a2, g1,
+        f2, f1, a1, g1,
     ):
         flow.step()
-    a2.step()
+    for flow in (a2, a2,):
+        flow.step()
     grad_in, grad_out = staged(
         feed_result_kernel, "feed_result", [shape((2, 512, 512), F32)] * 2,
         (info, *f2.chain.result(), *f1.chain.result(), *g1.chain.result()),
     )
-    a1.step()
-    a2.step()
+    for flow in (a1, a2,):
+        flow.step()
     (
         grad_query, grad_key, grad_value, grad_output, grad_b_in, gains, offsets, grad_b_out, norms
     ) = staged(

time: 260 us -> 257 us (0.988)
  starting transfers between devices: 64.9 us -> 57 us
    ppermute x69, starting transfers between devices: 64.9 us -> 57 us  [swap(): return lax.ppermute(value, axis, [(i, i ^ bit) for i in range(size)])]
    unnamed x106 -> x102, local copies, waits for them, and re-layouts: 7.21 us -> 7.61 us
  transfers between devices with their start and end apart: 69 -> 69, of which waited for: 29 -> 28; matrix products, arithmetic and copies ran while one was open for 0% -> 0% of each run, Pallas kernels for 33% -> 34%
where the time goes in v1:
time: 257 us; the launch traced here: 256 us
  Pallas kernels  114 us (44%)
  waiting for transfers between devices  74.3 us (29%)
  starting transfers between devices  57 us (22%)
  local copies, waits for them, and re-layouts  8.31 us (3%)
    pallas_call x11, Pallas kernels, staged(): pl.pallas_call(kernel, out_shape=tuple(out), in_specs=[pl.BlockSpec(memor...  92.4 us
    ppermute x69, waiting for transfers between devices, swap(): return lax.ppermute(value, axis, [(i, i ^ bit) for i in range(size)])  74.3 us
    ppermute x69, starting transfers between devices, swap(): return lax.ppermute(value, axis, [(i, i ^ bit) for i in range(size)])  57 us
    pallas_call x30, Pallas kernels, call(): pl.pallas_call(body, out_shape=tuple(out), in_specs=in_specs, out_specs=t...  15.1 us
    unnamed x102, local copies, waits for them, and re-layouts  7.61 us
  transfers between devices with their start and end apart: 69, of which 28 were waited for; matrix products, arithmetic and copies ran while one was open for 0% of the time, Pallas kernels for 34%

profile of v1, /device:TPU:0, one launch (start us, length us, event | category | flops | bytes accessed | tf_op | source)
XLA Modules:
  0.0 255.6 jit_solution(1176403422573189587)
XLA Ops:
  0.6 1.9 pack_first.1.refs_4_.refs_9_.refs_26_.refs_6_
  3.1 2.6 %collective-permute-start.1 = (bf16[512,512]{1,0:T(8,128)(2,1)}, bf16[512,512]{1,0:T(8,128)(2,1)S(1)}, u32[]{:S(2)}, u32[]{:S(2)}) collective-permute-start(bf16[512,512]{1,0:T(8,128)(2,1)} %pack_first.1.refs_4_.refs_9_.refs_26_.refs_6_), channel_id=1, source_target_pairs={{0,2},{1,3},{2,0},{3,1},{4,6},{5,7},{6,4},{7,5},{8,10},{9,11},{10,... | collective-permute-start | bytes 1572872 | tf_op jit(solution)/shard_map/ppermute | solution.py:1112
  7.0 4.3 %pack_rest.1 = (bf16[512,512]{1,0:T(8,128)(2,1)}, bf16[1056,512]{1,0:T(8,128)(2,1)}, bf16[528,512]{1,0:T(8,128)(2,1)}, bf16[1056,512]{1,0:T(8,128)(2,1)}, bf16[528,512]{1,0:T(8,128)(2,1)}) custom-call(s32[5]{0:T(128)} %stack.37.info_ref.refs_0_, bf16[2,512,128]{2,1,0:T(8,128)(2,1)} %wq.3, bf16[2,512,128]{2,1,0:T(8,128)(2,1)} %wk.3, bf16[2,512,128]{2,1,0:T(8,128)(2,1)} %wv.3, ...), custom_call_target="tpu_custom_call" | custom-call | tf_op jit(solution)/shard_map/pack_rest/pallas_call | solution.py:1092
  12.2 3.7 %first_near.1 = (bf16[256,512]{1,0:T(8,128)(2,1)}, f32[256,512]{1,0:T(8,128)}, bf16[2,512,384]{2,1,0:T(8,128)(2,1)}, bf16[2,80,256]{2,1,0:T(8,128)(2,1)}, bf16[2...) custom-call(s32[5]{0:T(128)} %stack.37.info_ref.refs_0_, bf16[1,256,512]{2,1,0:T(8,128)(2,1)} %refs_12_.3, ...), custom_call_target="tpu_custom_call" | custom-call | flops 1 | bytes 1 | tf_op jit(solution)/shard_map/first_near/pallas_call | solution.py:985
  15.8 2.8 %collective-permute-done.1.refs_2_.refs_11_.refs_28_.refs_8_ = bf16[512,512]{1,0:T(8,128)(2,1)S(1)} collective-permute-done((bf16[512,512]{1,0:T(8,128)(2,1)}, bf16[512,512]{1,0:T(8,128)(2,1)S(1)}, u32[]{:S(2)}, u32[]{:S(2)}) %collective-permute-start.1) | collective-permute-done | bytes 524320 | tf_op jit(solution)/shard_map/ppermute | solution.py:1112
  21.4 3.7 %first.1 = (bf16[2,512,384]{2,1,0:T(8,128)(2,1)}, bf16[4,80,256]{2,1,0:T(8,128)(2,1)}, bf16[4,96,256]{2,1,0:T(8,128)(2,1)}, bf16[4,16,256]{2,1,0:T(8,128)(2,1)}) custom-call(s32[5]{0:T(128)} %stack.37.info_ref.refs_0_, bf16[256,512]{1,0:T(8,128)(2,1)} %get-tuple-element.187.refs_1_.refs_5_, bf16[512,512]{1,0:T(8,128)(2,1)} %copy-done.17, ...), custom_call_target="tpu_custom_call" | custom-call | flops 1 | bytes 1 | tf_op jit(solution)/shard_map/first/pallas_call | solution.py:985
  25.1 1.8 collective-permute-start.5
  27.3 3.0 %collective-permute-done.8.refs_3_.refs_21_ = bf16[528,512]{1,0:T(8,128)(2,1)} collective-permute-done((bf16[528,512]{1,0:T(8,128)(2,1)}, bf16[528,512]{1,0:T(8,128)(2,1)}, u32[]{:S(2)}, u32[]{:S(2)}) %collective-permute-start.8) | collective-permute-done | bytes 540704 | tf_op jit(solution)/shard_map/ppermute | solution.py:1112
  30.3 1.9 collective-permute-start.9
  32.3 2.6 %collective-permute-done.6.refs_5_ = bf16[4,16,256]{2,1,0:T(8,128)(2,1)S(1)} collective-permute-done((bf16[4,16,256]{2,1,0:T(8,128)(2,1)}, bf16[4,16,256]{2,1,0:T(8,128)(2,1)S(1)}, u32[]{:S(2)}, u32[]{:S(2)}) %collective-permute-start.6) | collective-permute-done | bytes 32800 | tf_op jit(solution)/shard_map/ppermute | solution.py:1112
  34.9 1.8 collective-permute-start.13
  36.7 7.9 %mix.2 = (bf16[4,672,256]{2,1,0:T(8,128)(2,1)}, bf16[256,512]{1,0:T(8,128)(2,1)}, f32[256,512]{1,0:T(8,128)}, f32[256,512]{1,0:T(8,128)}, bf16[256,512]{1,0:T(8,128)(2,1)}, /*index=5*/f32[1,512]{1,0:T(1,128)}) custom-call(s32[5]{0:T(128)} %stack.37.info_ref.refs_0_, bf16[2,512,384]{2,1,0:T(8,128)(2,1)} %get-tuple-element.193.refs_1_.refs_33_, ...), custom_call_target="tpu_custom_call" | custom-call | flops 1 | bytes 1 | tf_op jit(solution)/shard_map/mix/pallas_call | solution.py:985
  46.9 4.5 %feed_near.1 = (bf16[2,256,512]{2,1,0:T(8,128)(2,1)}, bf16[2,256,512]{2,1,0:T(8,128)(2,1)}, f32[256,512]{1,0:T(8,128)}) custom-call(s32[5]{0:T(128)} %stack.37.info_ref.refs_0_, bf16[256,512]{1,0:T(8,128)(2,1)} %get-tuple-element.200.refs_1_.refs_17_, bf16[1056,512]{1,0:T(8,128)(2,1)} %get-tuple-element.202.refs_2_.refs_19_, bf16[1056,512]{1,0:T(8,128)(2,1)} %copy-done.23), custom_call_target="tpu_custom_call" | custom-call | flops 1 | bytes 1 | tf_op jit(solution)/shard_map/feed_near/pallas_call | solution.py:985
  51.8 1.7 collective-permute-done.14.refs_14_.refs_11_.refs_15_.refs_9_
  54.3 7.0 %feed.1 = (bf16[2,256,512]{2,1,0:T(8,128)(2,1)}, bf16[2,256,512]{2,1,0:T(8,128)(2,1)}, f32[2,512]{1,0:T(2,128)}, f32[256,512]{1,0:T(8,128)}, bf16[256,512]{1,0:T...) custom-call(s32[5]{0:T(128)} %stack.37.info_ref.refs_0_, ...), custom_call_target="tpu_custom_call" | custom-call | flops 1 | bytes 1 | tf_op jit(solution)/shard_map/feed/pallas_call | solution.py:985
  61.3 1.6 collective-permute-start.20
  62.8 1.4 collective-permute-start.16
  65.0 6.0 %collective-permute-done.17.refs_4_ = bf16[4,16,256]{2,1,0:T(8,128)(2,1)S(1)} collective-permute-done((bf16[4,16,256]{2,1,0:T(8,128)(2,1)}, bf16[4,16,256]{2,1,0:T(8,128)(2,1)S(1)}, u32[]{:S(2)}, u32[]{:S(2)}) %collective-permute-start.17) | collective-permute-done | bytes 32800 | tf_op jit(solution)/shard_map/ppermute | solution.py:1112
  71.7 7.7 %mix.3 = (bf16[4,672,256]{2,1,0:T(8,128)(2,1)}, bf16[256,512]{1,0:T(8,128)(2,1)}, f32[256,512]{1,0:T(8,128)}, f32[256,512]{1,0:T(8,128)}, bf16[256,512]{1,0:T(8,128)(2,1)}, /*index=5*/f32[1,512]{1,0:T(1,128)}) custom-call(s32[5]{0:T(128)} %stack.37.info_ref.refs_0_, bf16[4,512,384]{2,1,0:T(8,128)(2,1)} %get-tuple-element.214.refs_1_.refs_18_, ...), custom_call_target="tpu_custom_call" | custom-call | flops 1 | bytes 1 | tf_op jit(solution)/shard_map/mix/pallas_call | solution.py:985
  80.0 1.5 collective-permute-done.22.refs_8_
  82.4 21.5 %turn.1 = (f32[256,512]{1,0:T(8,128)}, f32[2,512]{1,0:T(2,128)}, bf16[8,128,512]{2,1,0:T(8,128)(2,1)}, bf16[8,128,512]{2,1,0:T(8,128)(2,1)}, bf16[8,128,512]{2,1...) custom-call(s32[5]{0:T(128)} %stack.37.info_ref.refs_0_, ...), custom_call_target="tpu_custom_call" | custom-call | flops 1 | bytes 1 | tf_op jit(solution)/shard_map/turn/pallas_call | solution.py:985
  104.3 1.1 collective-permute-start.25
  106.8 1.2 copy-done.2
  108.3 4.1 %collective-permute-done.26.refs_4_ = bf16[4,16,256]{2,1,0:T(8,128)(2,1)S(1)} collective-permute-done((bf16[4,16,256]{2,1,0:T(8,128)(2,1)}, bf16[4,16,256]{2,1,0:T(8,128)(2,1)S(1)}, u32[]{:S(2)}, u32[]{:S(2)}) %collective-permute-start.26) | collective-permute-done | bytes 32800 | tf_op jit(solution)/shard_map/ppermute | solution.py:1112
  112.5 1.4 collective-permute-start.28
  113.9 22.3 %between.1 = (bf16[8,64,512]{2,1,0:T(8,128)(2,1)}, bf16[8,64,512]{2,1,0:T(8,128)(2,1)}, bf16[8,64,512]{2,1,0:T(8,128)(2,1)}, bf16[8,64,512]{2,1,0:T(8,128)(2,1)}...) custom-call(s32[5]{0:T(128)} %stack.37.info_ref.refs_0_, ...), custom_call_target="tpu_custom_call" | custom-call | flops 1 | bytes 1 | tf_op jit(solution)/shard_map/between/pallas_call | solution.py:985
  137.6 1.3 collective-permute-start.32
  139.3 2.4 far_sum.5
  142.5 3.0 %collective-permute-done.32.refs_4_ = bf16[4,16,256]{2,1,0:T(8,128)(2,1)S(1)} collective-permute-done((bf16[4,16,256]{2,1,0:T(8,128)(2,1)}, bf16[4,16,256]{2,1,0:T(8,128)(2,1)S(1)}, u32[]{:S(2)}, u32[]{:S(2)}) %collective-permute-start.32) | collective-permute-done | bytes 32800 | tf_op jit(solution)/shard_map/ppermute | solution.py:1112
  146.1 1.2 core_sum.6
  148.0 6.5 %last.1 = (bf16[8,72,512]{2,1,0:T(8,128)(2,1)}, bf16[8,72,512]{2,1,0:T(8,128)(2,1)}, bf16[8,72,512]{2,1,0:T(8,128)(2,1)}, bf16[8,72,512]{2,1,0:T(8,128)(2,1)}, f32[256,512]{1,0:T(8,128)}) custom-call(s32[5]{0:T(128)} %stack.37.info_ref.refs_0_, bf16[4,256,384]{2,1,0:T(8,128)(2,1)} %get-tuple-element.261.refs_1_, bf16[4,80,256]{2,1,0:T(8,128)(2,1)} %copy-done.41, ...), custom_call_target="tpu_custom_call" | custom-call | flops 1 | bytes 1 | tf_op jit(solution)/shard_map/last/pallas_call | solution.py:985
  155.1 1.2 core_sum.7
  156.3 1.5 collective-permute-start.39
  157.8 1.8 collective-permute-done.34.arrived_ref
  159.6 2.6 %collective-permute-done.36.back_ref = bf16[8,64,512]{2,1,0:T(8,128)(2,1)S(1)} collective-permute-done((bf16[8,64,512]{2,1,0:T(8,128)(2,1)S(1)}, bf16[8,64,512]{2,1,0:T(8,128)(2,1)S(1)}, u32[]{:S(2)}, u32[]{:S(2)}) %collective-permute-start.36) | collective-permute-done | bytes 524320 | tf_op jit(solution)/shard_map/ppermute | solution.py:1112
  162.9 1.3 far_sum.6
  164.7 1.6 collective-permute-start.40
  166.3 7.1 %collective-permute-done.39.back_ref = bf16[8,64,512]{2,1,0:T(8,128)(2,1)S(1)} collective-permute-done((bf16[8,64,512]{2,1,0:T(8,128)(2,1)S(1)}, bf16[8,64,512]{2,1,0:T(8,128)(2,1)S(1)}, u32[]{:S(2)}, u32[]{:S(2)}) %collective-permute-start.39) | collective-permute-done | bytes 524320 | tf_op jit(solution)/shard_map/ppermute | solution.py:1112
  173.4 1.5 collective-permute-start.41
  175.8 4.0 %collective-permute-done.41.arrived_ref = bf16[4,64,512]{2,1,0:T(8,128)(2,1)S(1)} collective-permute-done((bf16[4,64,512]{2,1,0:T(8,128)(2,1)S(1)}, bf16[4,64,512]{2,1,0:T(8,128)(2,1)S(1)}, u32[]{:S(2)}, u32[]{:S(2)}) %collective-permute-start.41) | collective-permute-done | bytes 262176 | tf_op jit(solution)/shard_map/ppermute | solution.py:1112
  180.9 1.5 collective-permute-start.45
  182.4 2.6 %collective-permute-start.47 = (bf16[2,128,512]{2,1,0:T(8,128)(2,1)S(1)}, bf16[2,128,512]{2,1,0:T(8,128)(2,1)S(1)}, u32[]{:S(2)}, u32[]{:S(2)}) collective-permute-start(bf16[2,128,512]{2,1,0:T(8,128)(2,1)S(1)} %add.33.stay_ref), channel_id=1, source_target_pairs={{0,16},{4,20},{8,24},{12,28},{16,0},{20,4},{24,8},{28,12},{1,17},{... | collective-permute-start | bytes 786440 | tf_op jit(solution)/shard_map/ppermute | solution.py:1112
  186.0 1.6 collective-permute-start.46
  188.4 1.6 collective-permute-start.50
  190.6 1.2 collective-permute-done.46.arrived_ref
  191.8 2.2 collective-permute-done.47.arrived_ref
  194.8 1.4 collective-permute-start.51
  196.9 1.4 collective-permute-start.55
  198.9 1.6 collective-permute-start.53
  200.6 5.5 %collective-permute-done.51.arrived_ref = bf16[2,64,512]{2,1,0:T(8,128)(2,1)S(1)} collective-permute-done((bf16[2,64,512]{2,1,0:T(8,128)(2,1)S(1)}, bf16[2,64,512]{2,1,0:T(8,128)(2,1)S(1)}, u32[]{:S(2)}, u32[]{:S(2)}) %collective-permute-start.51) | collective-permute-done | bytes 131104 | tf_op jit(solution)/shard_map/ppermute | solution.py:1112
  206.1 3.0 %collective-permute-start.54 = (bf16[2,64,512]{2,1,0:T(8,128)(2,1)S(1)}, bf16[2,64,512]{2,1,0:T(8,128)(2,1)S(1)}, u32[]{:S(2)}, u32[]{:S(2)}) collective-permute-start(bf16[2,64,512]{2,1,0:T(8,128)(2,1)S(1)} %add.36.stay_ref), channel_id=1, source_target_pairs={{0,16},{4,20},{8,24},{12,28},{16,0},{20,4},{24,8},{28,12},{1,17},{... | collective-permute-start | bytes 393224 | tf_op jit(solution)/shard_map/ppermute | solution.py:1112
  211.0 2.3 collective-permute-start.58
  213.3 4.1 %collective-permute-done.54.arrived_ref = bf16[2,64,512]{2,1,0:T(8,128)(2,1)S(1)} collective-permute-done((bf16[2,64,512]{2,1,0:T(8,128)(2,1)S(1)}, bf16[2,64,512]{2,1,0:T(8,128)(2,1)S(1)}, u32[]{:S(2)}, u32[]{:S(2)}) %collective-permute-start.54) | collective-permute-done | bytes 131104 | tf_op jit(solution)/shard_map/ppermute | solution.py:1112
  218.2 2.1 collective-permute-start.59
  220.8 5.5 %collective-permute-done.57.other_ref = bf16[2,64,512]{2,1,0:T(8,128)(2,1)S(1)} collective-permute-done((bf16[2,64,512]{2,1,0:T(8,128)(2,1)S(1)}, bf16[2,64,512]{2,1,0:T(8,128)(2,1)S(1)}, u32[]{:S(2)}, u32[]{:S(2)}) %collective-permute-start.57) | collective-permute-done | bytes 131104 | tf_op jit(solution)/shard_map/ppermute | solution.py:1112
  227.0 1.0 collective-permute-done.59.arrived_ref
  228.1 1.4 collective-permute-done.60.other_ref
  230.7 3.2 %collective-permute-start.65 = (bf16[2,64,512]{2,1,0:T(8,128)(2,1)S(1)}, bf16[2,64,512]{2,1,0:T(8,128)(2,1)S(1)}, u32[]{:S(2)}, u32[]{:S(2)}) collective-permute-start(bf16[2,64,512]{2,1,0:T(8,128)(2,1)S(1)} %add.41.stay_ref), channel_id=1, source_target_pairs={{0,16},{4,20},{8,24},{12,28},{16,0},{20,4},{24,8},{28,12},{1,17},{... | collective-permute-start | bytes 393224 | tf_op jit(solution)/shard_map/ppermute | solution.py:1112
  233.9 3.2 %collective-permute-done.63.other_ref = bf16[2,72,512]{2,1,0:T(8,128)(2,1)S(1)} collective-permute-done((bf16[2,72,512]{2,1,0:T(8,128)(2,1)S(1)}, bf16[2,72,512]{2,1,0:T(8,128)(2,1)S(1)}, u32[]{:S(2)}, u32[]{:S(2)}) %collective-permute-start.63) | collective-permute-done | bytes 147488 | tf_op jit(solution)/shard_map/ppermute | solution.py:1112
  237.7 1.6 collective-permute-done.64.refs_6_
  240.2 4.1 %collective-permute-done.66.other_ref = bf16[2,64,512]{2,1,0:T(8,128)(2,1)S(1)} collective-permute-done((bf16[2,64,512]{2,1,0:T(8,128)(2,1)S(1)}, bf16[2,64,512]{2,1,0:T(8,128)(2,1)S(1)}, u32[]{:S(2)}, u32[]{:S(2)}) %collective-permute-start.66) | collective-permute-done | bytes 131104 | tf_op jit(solution)/shard_map/ppermute | solution.py:1112
  245.7 4.4 %feed_result.1 = (f32[2,512,512]{2,1,0:T(8,128)}, f32[2,512,512]{2,1,0:T(8,128)}) custom-call(s32[5]{0:T(128)} %stack.37.info_ref.refs_0_, bf16[4,128,512]{2,1,0:T(8,128)(2,1)} %copy-done, bf16[4,128,512]{2,1,0:T(8,128)(2,1)} %copy-done.31, bf16[4,64,512]{2,1,0:T(8,128)(2,1)} %copy-done.3, bf16[4,64,512]{2,1,0:T(8,128)(2,1)} %copy-done.33, ...), custom_call_target="tpu_custom_call" | custom-call | flops 1 | bytes 1 | tf_op jit(solution)/shard_map/feed_result/pallas_call | solution.py:985
  250.1 1.3 collective-permute-done.68.refs_4_
  252.1 3.3 %attn_result.1 = (f32[2,512,128]{2,1,0:T(8,128)}, f32[2,512,128]{2,1,0:T(8,128)}, f32[2,512,128]{2,1,0:T(8,128)}, f32[2,128,512]{2,1,0:T(8,128)}, f32[2,512]{1,0...) custom-call(s32[5]{0:T(128)} %stack.37.info_ref.refs_0_, ...), custom_call_target="tpu_custom_call" | custom-call | flops 1 | bytes 1 | tf_op jit(solution)/shard_map/attn_result/pallas_call | solution.py:985
  (222 shorter events, 34.6 us)
Async XLA Ops:
  2.5 8.8 %collective-permute-start = (bf16[512,512]{1,0:T(8,128)(2,1)}, bf16[512,512]{1,0:T(8,128)(2,1)S(1)}, u32[]{:S(2)}, u32[]{:S(2)}) collective-permute-start(bf16[512,512]{1,0:T(8,128)(2,1)} %pack_first.1.refs_4_.refs_9_.refs_26_.refs_6_), channel_id=1, source_target_pairs={{0,1},{1,0},{2,3},{3,2},{4,5},{5,4},{6,7},{7,6},{8,9},{9,8},{10,11... | collective-permute-start | bytes 1572872 | tf_op jit(solution)/shard_map/ppermute | solution.py:1112
  3.1 15.6 %collective-permute-start.1 = (bf16[512,512]{1,0:T(8,128)(2,1)}, bf16[512,512]{1,0:T(8,128)(2,1)S(1)}, u32[]{:S(2)}, u32[]{:S(2)}) collective-permute-start(bf16[512,512]{1,0:T(8,128)(2,1)} %pack_first.1.refs_4_.refs_9_.refs_26_.refs_6_), channel_id=1, source_target_pairs={{0,2},{1,3},{2,0},{3,1},{4,6},{5,7},{6,4},{7,5},{8,10},{9,11},{10,... | collective-permute-start | bytes 1572872 | tf_op jit(solution)/shard_map/ppermute | solution.py:1112
  11.3 19.1 %collective-permute-start.8 = (bf16[528,512]{1,0:T(8,128)(2,1)}, bf16[528,512]{1,0:T(8,128)(2,1)}, u32[]{:S(2)}, u32[]{:S(2)}) collective-permute-start(bf16[528,512]{1,0:T(8,128)(2,1)} %get-tuple-element.183), channel_id=1, source_target_pairs={{0,2},{1,3},{2,0},{3,1},{4,6},{5,7},{6,4},{7,5},{8,10},{9,11},{10,... | collective-permute-start | bytes 1622024 | tf_op jit(solution)/shard_map/ppermute | solution.py:1112
  11.4 34.5 %collective-permute-start.7 = (bf16[1056,512]{1,0:T(8,128)(2,1)}, bf16[1056,512]{1,0:T(8,128)(2,1)S(1)}, u32[]{:S(2)}, u32[]{:S(2)}) collective-permute-start(bf16[1056,512]{1,0:T(8,128)(2,1)} %get-tuple-element.202.refs_2_.refs_19_), channel_id=1, source_target_pairs={{0,1},{1,0},{2,3},{3,2},{4,5},{5,4},{6,7},{7,6},{8,9},{9,8},{10,11... | collective-permute-start | bytes 3244040 | tf_op jit(solution)/shard_map/ppermute | solution.py:1112
  25.1 9.8 %collective-permute-start.5 = (bf16[4,96,256]{2,1,0:T(8,128)(2,1)}, bf16[4,96,256]{2,1,0:T(8,128)(2,1)S(1)}, u32[]{:S(2)}, u32[]{:S(2)}) collective-permute-start(bf16[4,96,256]{2,1,0:T(8,128)(2,1)} %get-tuple-element.196), channel_id=1, source_target_pairs={{0,3},{1,2},{2,1},{3,0},{4,7},{5,6},{6,5},{7,4},{8,11},{9,10},{10,... | collective-permute-start | bytes 589832 | tf_op jit(solution)/shard_map/ppermute | solution.py:1112
  26.8 3.5 %collective-permute-start.4 = (bf16[4,80,256]{2,1,0:T(8,128)(2,1)}, bf16[4,80,256]{2,1,0:T(8,128)(2,1)S(1)}, u32[]{:S(2)}, u32[]{:S(2)}) collective-permute-start(bf16[4,80,256]{2,1,0:T(8,128)(2,1)} %get-tuple-element.195), channel_id=1, source_target_pairs={{0,1},{1,0},{2,3},{3,2},{4,5},{5,4},{6,7},{7,6},{8,9},{9,8},{10,11... | collective-permute-start | bytes 491528 | tf_op jit(solution)/shard_map/ppermute | solution.py:1112
  27.2 7.7 %collective-permute-start.6 = (bf16[4,16,256]{2,1,0:T(8,128)(2,1)}, bf16[4,16,256]{2,1,0:T(8,128)(2,1)S(1)}, u32[]{:S(2)}, u32[]{:S(2)}) collective-permute-start(bf16[4,16,256]{2,1,0:T(8,128)(2,1)} %get-tuple-element.191), channel_id=1, source_target_pairs={{0,2},{1,3},{2,0},{3,1},{4,6},{5,7},{6,4},{7,5},{8,10},{9,11},{10,... | collective-permute-start | bytes 98312 | tf_op jit(solution)/shard_map/ppermute | solution.py:1112
  30.3 14.3 %collective-permute-start.9 = (bf16[528,512]{1,0:T(8,128)(2,1)}, bf16[528,512]{1,0:T(8,128)(2,1)S(1)}, u32[]{:S(2)}, u32[]{:S(2)}) collective-permute-start(bf16[528,512]{1,0:T(8,128)(2,1)} %collective-permute-done.8.refs_3_.refs_21_), channel_id=1, source_target_pairs={{0,4},{4,0},{8,12},{12,8},{16,20},{20,16},{24,28},{28,24},{1,5},{5... | collective-permute-start | bytes 1622024 | tf_op jit(solution)/shard_map/ppermute | solution.py:1112
  34.9 16.6 %collective-permute-start.13 = (bf16[512,512]{1,0:T(8,128)(2,1)S(1)}, bf16[512,512]{1,0:T(8,128)(2,1)S(1)}, u32[]{:S(2)}, u32[]{:S(2)}) collective-permute-start(bf16[512,512]{1,0:T(8,128)(2,1)S(1)} %copy-done.19), channel_id=1, source_target_pairs={{0,2},{1,3},{2,0},{3,1},{4,6},{5,7},{6,4},{7,5},{8,10},{9,11},{10,... | collective-permute-start | bytes 1572872 | tf_op jit(solution)/shard_map/ppermute | solution.py:1112
  36.7 15.1 %collective-permute-start.10 = (bf16[528,512]{1,0:T(8,128)(2,1)}, bf16[528,512]{1,0:T(8,128)(2,1)}, u32[]{:S(2)}, u32[]{:S(2)}) collective-permute-start(bf16[528,512]{1,0:T(8,128)(2,1)} %collective-permute-done.8.refs_3_.refs_21_), channel_id=1, source_target_pairs={{0,1},{1,0},{2,3},{3,2},{4,5},{5,4},{6,7},{7,6},{8,9},{9,8},{10,11... | collective-permute-start | bytes 1622024 | tf_op jit(solution)/shard_map/ppermute | solution.py:1112
  44.6 7.2 %collective-permute-start.11 = (bf16[528,512]{1,0:T(8,128)(2,1)S(1)}, bf16[528,512]{1,0:T(8,128)(2,1)}, u32[]{:S(2)}, u32[]{:S(2)}) collective-permute-start(bf16[528,512]{1,0:T(8,128)(2,1)S(1)} %collective-permute-done.9.refs_4_.refs_22_), channel_id=1, source_target_pairs={{0,1},{1,0},{2,3},{3,2},{4,5},{5,4},{6,7},{7,6},{8,9},{9,8},{10,11... | collective-permute-start | bytes 1622024 | tf_op jit(solution)/shard_map/ppermute | solution.py:1112
  45.2 16.1 %collective-permute-start.19 = (bf16[528,512]{1,0:T(8,128)(2,1)}, bf16[528,512]{1,0:T(8,128)(2,1)}, u32[]{:S(2)}, u32[]{:S(2)}) collective-permute-start(bf16[528,512]{1,0:T(8,128)(2,1)} %get-tuple-element.225), channel_id=1, source_target_pairs={{0,2},{1,3},{2,0},{3,1},{4,6},{5,7},{6,4},{7,5},{8,10},{9,11},{10,... | collective-permute-start | bytes 1622024 | tf_op jit(solution)/shard_map/ppermute | solution.py:1112
  45.9 5.9 %collective-permute-start.12 = (bf16[512,512]{1,0:T(8,128)(2,1)S(1)}, bf16[512,512]{1,0:T(8,128)(2,1)S(1)}, u32[]{:S(2)}, u32[]{:S(2)}) collective-permute-start(bf16[512,512]{1,0:T(8,128)(2,1)S(1)} %copy-done.19), channel_id=1, source_target_pairs={{0,1},{1,0},{2,3},{3,2},{4,5},{5,4},{6,7},{7,6},{8,9},{9,8},{10,11... | collective-permute-start | bytes 1572872 | tf_op jit(solution)/shard_map/ppermute | solution.py:1112
  61.3 18.2 %collective-permute-start.20 = (bf16[528,512]{1,0:T(8,128)(2,1)}, bf16[528,512]{1,0:T(8,128)(2,1)S(1)}, u32[]{:S(2)}, u32[]{:S(2)}) collective-permute-start(bf16[528,512]{1,0:T(8,128)(2,1)} %collective-permute-done.19.refs_5_), channel_id=1, source_target_pairs={{0,4},{4,0},{8,12},{12,8},{16,20},{20,16},{24,28},{28,24},{1,5},{5... | collective-permute-start | bytes 1622024 | tf_op jit(solution)/shard_map/ppermute | solution.py:1112
  62.8 17.2 %collective-permute-start.18 = (bf16[1056,512]{1,0:T(8,128)(2,1)}, bf16[1056,512]{1,0:T(8,128)(2,1)S(1)}, u32[]{:S(2)}, u32[]{:S(2)}) collective-permute-start(bf16[1056,512]{1,0:T(8,128)(2,1)} %get-tuple-element.223.refs_3_), channel_id=1, source_target_pairs={{0,1},{1,0},{2,3},{3,2},{4,5},{5,4},{6,7},{7,6},{8,9},{9,8},{10,11... | collective-permute-start | bytes 3244040 | tf_op jit(solution)/shard_map/ppermute | solution.py:1112
  62.8 8.1 %collective-permute-start.16 = (bf16[4,96,256]{2,1,0:T(8,128)(2,1)}, bf16[4,96,256]{2,1,0:T(8,128)(2,1)S(1)}, u32[]{:S(2)}, u32[]{:S(2)}) collective-permute-start(bf16[4,96,256]{2,1,0:T(8,128)(2,1)} %get-tuple-element.216), channel_id=1, source_target_pairs={{0,3},{1,2},{2,1},{3,0},{4,7},{5,6},{6,5},{7,4},{8,11},{9,10},{10,... | collective-permute-start | bytes 589832 | tf_op jit(solution)/shard_map/ppermute | solution.py:1112
  64.3 6.7 %collective-permute-start.15 = (bf16[4,80,256]{2,1,0:T(8,128)(2,1)}, bf16[4,80,256]{2,1,0:T(8,128)(2,1)S(1)}, u32[]{:S(2)}, u32[]{:S(2)}) collective-permute-start(bf16[4,80,256]{2,1,0:T(8,128)(2,1)} %get-tuple-element.215), channel_id=1, source_target_pairs={{0,1},{1,0},{2,3},{3,2},{4,5},{5,4},{6,7},{7,6},{8,9},{9,8},{10,11... | collective-permute-start | bytes 491528 | tf_op jit(solution)/shard_map/ppermute | solution.py:1112
  64.3 6.7 %collective-permute-start.17 = (bf16[4,16,256]{2,1,0:T(8,128)(2,1)}, bf16[4,16,256]{2,1,0:T(8,128)(2,1)S(1)}, u32[]{:S(2)}, u32[]{:S(2)}) collective-permute-start(bf16[4,16,256]{2,1,0:T(8,128)(2,1)} %get-tuple-element.212), channel_id=1, source_target_pairs={{0,2},{1,3},{2,0},{3,1},{4,6},{5,7},{6,4},{7,5},{8,10},{9,11},{10,... | collective-permute-start | bytes 98312 | tf_op jit(solution)/shard_map/ppermute | solution.py:1112
  70.9 9.1 %collective-permute-start.21 = (bf16[528,512]{1,0:T(8,128)(2,1)}, bf16[528,512]{1,0:T(8,128)(2,1)S(1)}, u32[]{:S(2)}, u32[]{:S(2)}) collective-permute-start(bf16[528,512]{1,0:T(8,128)(2,1)} %collective-permute-done.19.refs_5_), channel_id=1, source_target_pairs={{0,1},{1,0},{2,3},{3,2},{4,5},{5,4},{6,7},{7,6},{8,9},{9,8},{10,11... | collective-permute-start | bytes 1622024 | tf_op jit(solution)/shard_map/ppermute | solution.py:1112
  103.9 2.9 %collective-permute-start.23 = (bf16[8,128,512]{2,1,0:T(8,128)(2,1)}, bf16[8,128,512]{2,1,0:T(8,128)(2,1)S(1)}, u32[]{:S(2)}, u32[]{:S(2)}) collective-permute-start(bf16[8,128,512]{2,1,0:T(8,128)(2,1)} %get-tuple-element.236), channel_id=1, source_target_pairs={{0,1},{1,0},{2,3},{3,2},{4,5},{5,4},{6,7},{7,6},{8,9},{9,8},{10,11... | collective-permute-start | bytes 3145736 | tf_op jit(solution)/shard_map/ppermute | solution.py:1112
  104.3 8.1 %collective-permute-start.25 = (bf16[4,96,256]{2,1,0:T(8,128)(2,1)}, bf16[4,96,256]{2,1,0:T(8,128)(2,1)S(1)}, u32[]{:S(2)}, u32[]{:S(2)}) collective-permute-start(bf16[4,96,256]{2,1,0:T(8,128)(2,1)} %get-tuple-element.240), channel_id=1, source_target_pairs={{0,3},{1,2},{2,1},{3,0},{4,7},{5,6},{6,5},{7,4},{8,11},{9,10},{10,... | collective-permute-start | bytes 589832 | tf_op jit(solution)/shard_map/ppermute | solution.py:1112
  105.4 7.0 %collective-permute-start.24 = (bf16[4,80,256]{2,1,0:T(8,128)(2,1)}, bf16[4,80,256]{2,1,0:T(8,128)(2,1)S(1)}, u32[]{:S(2)}, u32[]{:S(2)}) collective-permute-start(bf16[4,80,256]{2,1,0:T(8,128)(2,1)} %get-tuple-element.239), channel_id=1, source_target_pairs={{0,1},{1,0},{2,3},{3,2},{4,5},{5,4},{6,7},{7,6},{8,9},{9,8},{10,11... | collective-permute-start | bytes 491528 | tf_op jit(solution)/shard_map/ppermute | solution.py:1112
  105.8 6.7 %collective-permute-start.26 = (bf16[4,16,256]{2,1,0:T(8,128)(2,1)}, bf16[4,16,256]{2,1,0:T(8,128)(2,1)S(1)}, u32[]{:S(2)}, u32[]{:S(2)}) collective-permute-start(bf16[4,16,256]{2,1,0:T(8,128)(2,1)} %get-tuple-element.234), channel_id=1, source_target_pairs={{0,2},{1,3},{2,0},{3,1},{4,6},{5,7},{6,4},{7,5},{8,10},{9,11},{10,... | collective-permute-start | bytes 98312 | tf_op jit(solution)/shard_map/ppermute | solution.py:1112
  112.5 24.9 %collective-permute-start.28 = (bf16[8,128,512]{2,1,0:T(8,128)(2,1)S(1)}, bf16[8,128,512]{2,1,0:T(8,128)(2,1)S(1)}, u32[]{:S(2)}, u32[]{:S(2)}) collective-permute-start(bf16[8,128,512]{2,1,0:T(8,128)(2,1)S(1)} %core_sum.5), channel_id=1, source_target_pairs={{0,2},{1,3},{2,0},{3,1},{4,6},{5,7},{6,4},{7,5},{8,10},{9,11},{10,... | collective-permute-start | bytes 3145736 | tf_op jit(solution)/shard_map/ppermute | solution.py:1112
  113.9 23.8 %collective-permute-start.27 = (bf16[8,128,512]{2,1,0:T(8,128)(2,1)}, bf16[8,128,512]{2,1,0:T(8,128)(2,1)}, u32[]{:S(2)}, u32[]{:S(2)}) collective-permute-start(bf16[8,128,512]{2,1,0:T(8,128)(2,1)} %get-tuple-element.255), channel_id=1, source_target_pairs={{0,1},{1,0},{2,3},{3,2},{4,5},{5,4},{6,7},{7,6},{8,9},{9,8},{10,11... | collective-permute-start | bytes 3145736 | tf_op jit(solution)/shard_map/ppermute | solution.py:1112
  136.7 17.9 %collective-permute-start.33 = (bf16[8,64,512]{2,1,0:T(8,128)(2,1)}, bf16[8,64,512]{2,1,0:T(8,128)(2,1)}, u32[]{:S(2)}, u32[]{:S(2)}) collective-permute-start(bf16[8,64,512]{2,1,0:T(8,128)(2,1)} %get-tuple-element.278), channel_id=1, source_target_pairs={{0,1},{1,0},{2,3},{3,2},{4,5},{5,4},{6,7},{7,6},{8,9},{9,8},{10,11... | collective-permute-start | bytes 1572872 | tf_op jit(solution)/shard_map/ppermute | solution.py:1112
  136.8 19.5 %collective-permute-start.35 = (bf16[8,64,512]{2,1,0:T(8,128)(2,1)}, bf16[8,64,512]{2,1,0:T(8,128)(2,1)}, u32[]{:S(2)}, u32[]{:S(2)}) collective-permute-start(bf16[8,64,512]{2,1,0:T(8,128)(2,1)} %get-tuple-element.286), channel_id=1, source_target_pairs={{0,1},{1,0},{2,3},{3,2},{4,5},{5,4},{6,7},{7,6},{8,9},{9,8},{10,11... | collective-permute-start | bytes 1572872 | tf_op jit(solution)/shard_map/ppermute | solution.py:1112
  137.4 9.8 %collective-permute-start.31 = (bf16[4,96,256]{2,1,0:T(8,128)(2,1)}, bf16[4,96,256]{2,1,0:T(8,128)(2,1)S(1)}, u32[]{:S(2)}, u32[]{:S(2)}) collective-permute-start(bf16[4,96,256]{2,1,0:T(8,128)(2,1)} %get-tuple-element.265), channel_id=1, source_target_pairs={{0,3},{1,2},{2,1},{3,0},{4,7},{5,6},{6,5},{7,4},{8,11},{9,10},{10,... | collective-permute-start | bytes 589832 | tf_op jit(solution)/shard_map/ppermute | solution.py:1112
  137.6 7.9 %collective-permute-start.32 = (bf16[4,16,256]{2,1,0:T(8,128)(2,1)}, bf16[4,16,256]{2,1,0:T(8,128)(2,1)S(1)}, u32[]{:S(2)}, u32[]{:S(2)}) collective-permute-start(bf16[4,16,256]{2,1,0:T(8,128)(2,1)} %get-tuple-element.266), channel_id=1, source_target_pairs={{0,2},{1,3},{2,0},{3,1},{4,6},{5,7},{6,4},{7,5},{8,10},{9,11},{10,... | collective-permute-start | bytes 98312 | tf_op jit(solution)/shard_map/ppermute | solution.py:1112
  139.0 8.3 %collective-permute-start.30 = (bf16[4,80,256]{2,1,0:T(8,128)(2,1)}, bf16[4,80,256]{2,1,0:T(8,128)(2,1)S(1)}, u32[]{:S(2)}, u32[]{:S(2)}) collective-permute-start(bf16[4,80,256]{2,1,0:T(8,128)(2,1)} %get-tuple-element.263), channel_id=1, source_target_pairs={{0,1},{1,0},{2,3},{3,2},{4,5},{5,4},{6,7},{7,6},{8,9},{9,8},{10,11... | collective-permute-start | bytes 491528 | tf_op jit(solution)/shard_map/ppermute | solution.py:1112
  145.5 14.1 %collective-permute-start.34 = (bf16[4,128,512]{2,1,0:T(8,128)(2,1)}, bf16[4,128,512]{2,1,0:T(8,128)(2,1)S(1)}, u32[]{:S(2)}, u32[]{:S(2)}) collective-permute-start(bf16[4,128,512]{2,1,0:T(8,128)(2,1)} %get-tuple-element.257), channel_id=1, source_target_pairs={{0,4},{4,0},{8,12},{12,8},{16,20},{20,16},{24,28},{28,24},{1,5},{5... | collective-permute-start | bytes 1572872 | tf_op jit(solution)/shard_map/ppermute | solution.py:1112
  147.3 14.9 %collective-permute-start.36 = (bf16[8,64,512]{2,1,0:T(8,128)(2,1)S(1)}, bf16[8,64,512]{2,1,0:T(8,128)(2,1)S(1)}, u32[]{:S(2)}, u32[]{:S(2)}) collective-permute-start(bf16[8,64,512]{2,1,0:T(8,128)(2,1)S(1)} %core_sum.6), channel_id=1, source_target_pairs={{0,2},{1,3},{2,0},{3,1},{4,6},{5,7},{6,4},{7,5},{8,10},{9,11},{10,... | collective-permute-start | bytes 1572872 | tf_op jit(solution)/shard_map/ppermute | solution.py:1112
  154.5 9.7 %collective-permute-start.37 = (bf16[8,72,512]{2,1,0:T(8,128)(2,1)}, bf16[8,72,512]{2,1,0:T(8,128)(2,1)S(1)}, u32[]{:S(2)}, u32[]{:S(2)}) collective-permute-start(bf16[8,72,512]{2,1,0:T(8,128)(2,1)} %get-tuple-element.290), channel_id=1, source_target_pairs={{0,1},{1,0},{2,3},{3,2},{4,5},{5,4},{6,7},{7,6},{8,9},{9,8},{10,11... | collective-permute-start | bytes 1769480 | tf_op jit(solution)/shard_map/ppermute | solution.py:1112
  154.6 10.1 %collective-permute-start.38 = (bf16[8,64,512]{2,1,0:T(8,128)(2,1)S(1)}, bf16[8,64,512]{2,1,0:T(8,128)(2,1)S(1)}, u32[]{:S(2)}, u32[]{:S(2)}) collective-permute-start(bf16[8,64,512]{2,1,0:T(8,128)(2,1)S(1)} %copy-done.50), channel_id=1, source_target_pairs={{0,1},{1,0},{2,3},{3,2},{4,5},{5,4},{6,7},{7,6},{8,9},{9,8},{10,11... | collective-permute-start | bytes 1572872 | tf_op jit(solution)/shard_map/ppermute | solution.py:1112
  156.3 17.1 %collective-permute-start.39 = (bf16[8,64,512]{2,1,0:T(8,128)(2,1)S(1)}, bf16[8,64,512]{2,1,0:T(8,128)(2,1)S(1)}, u32[]{:S(2)}, u32[]{:S(2)}) collective-permute-start(bf16[8,64,512]{2,1,0:T(8,128)(2,1)S(1)} %core_sum.7), channel_id=1, source_target_pairs={{0,2},{1,3},{2,0},{3,1},{4,6},{5,7},{6,4},{7,5},{8,10},{9,11},{10,... | collective-permute-start | bytes 1572872 | tf_op jit(solution)/shard_map/ppermute | solution.py:1112
  159.6 20.8 %collective-permute-start.42 = (bf16[8,64,512]{2,1,0:T(8,128)(2,1)S(1)}, bf16[8,64,512]{2,1,0:T(8,128)(2,1)S(1)}, u32[]{:S(2)}, u32[]{:S(2)}) collective-permute-start(bf16[8,64,512]{2,1,0:T(8,128)(2,1)S(1)} %copy-done.49), channel_id=1, source_target_pairs={{0,1},{1,0},{2,3},{3,2},{4,5},{5,4},{6,7},{7,6},{8,9},{9,8},{10,11... | collective-permute-start | bytes 1572872 | tf_op jit(solution)/shard_map/ppermute | solution.py:1112
  162.2 20.3 %collective-permute-start.43 = (bf16[8,72,512]{2,1,0:T(8,128)(2,1)}, bf16[8,72,512]{2,1,0:T(8,128)(2,1)S(1)}, u32[]{:S(2)}, u32[]{:S(2)}) collective-permute-start(bf16[8,72,512]{2,1,0:T(8,128)(2,1)} %get-tuple-element.304), channel_id=1, source_target_pairs={{0,1},{1,0},{2,3},{3,2},{4,5},{5,4},{6,7},{7,6},{8,9},{9,8},{10,11... | collective-permute-start | bytes 1769480 | tf_op jit(solution)/shard_map/ppermute | solution.py:1112
  164.4 21.7 %collective-permute-start.44 = (bf16[8,72,512]{2,1,0:T(8,128)(2,1)S(1)}, bf16[8,72,512]{2,1,0:T(8,128)(2,1)S(1)}, u32[]{:S(2)}, u32[]{:S(2)}) collective-permute-start(bf16[8,72,512]{2,1,0:T(8,128)(2,1)S(1)} %core_sum.8), channel_id=1, source_target_pairs={{0,2},{1,3},{2,0},{3,1},{4,6},{5,7},{6,4},{7,5},{8,10},{9,11},{10,... | collective-permute-start | bytes 1769480 | tf_op jit(solution)/shard_map/ppermute | solution.py:1112
  164.7 10.9 %collective-permute-start.40 = (bf16[2,128,512]{2,1,0:T(8,128)(2,1)S(1)}, bf16[2,128,512]{2,1,0:T(8,128)(2,1)S(1)}, u32[]{:S(2)}, u32[]{:S(2)}) collective-permute-start(bf16[2,128,512]{2,1,0:T(8,128)(2,1)S(1)} %get-tuple-element.283), channel_id=1, source_target_pairs={{0,8},{4,12},{8,0},{12,4},{16,24},{20,28},{24,16},{28,20},{1,9},{5... | collective-permute-start | bytes 786440 | tf_op jit(solution)/shard_map/ppermute | solution.py:1112
  173.4 6.4 %collective-permute-start.41 = (bf16[4,64,512]{2,1,0:T(8,128)(2,1)S(1)}, bf16[4,64,512]{2,1,0:T(8,128)(2,1)S(1)}, u32[]{:S(2)}, u32[]{:S(2)}) collective-permute-start(bf16[4,64,512]{2,1,0:T(8,128)(2,1)S(1)} %get-tuple-element.288), channel_id=1, source_target_pairs={{0,4},{4,0},{8,12},{12,8},{16,20},{20,16},{24,28},{28,24},{1,5},{5... | collective-permute-start | bytes 786440 | tf_op jit(solution)/shard_map/ppermute | solution.py:1112
  175.7 20.5 %collective-permute-start.48 = (bf16[8,64,512]{2,1,0:T(8,128)(2,1)S(1)}, bf16[8,64,512]{2,1,0:T(8,128)(2,1)S(1)}, u32[]{:S(2)}, u32[]{:S(2)}) collective-permute-start(bf16[8,64,512]{2,1,0:T(8,128)(2,1)S(1)} %copy-done.48), channel_id=1, source_target_pairs={{0,1},{1,0},{2,3},{3,2},{4,5},{5,4},{6,7},{7,6},{8,9},{9,8},{10,11... | collective-permute-start | bytes 1572872 | tf_op jit(solution)/shard_map/ppermute | solution.py:1112
  180.5 15.6 %collective-permute-start.49 = (bf16[8,64,512]{2,1,0:T(8,128)(2,1)S(1)}, bf16[8,64,512]{2,1,0:T(8,128)(2,1)S(1)}, u32[]{:S(2)}, u32[]{:S(2)}) collective-permute-start(bf16[8,64,512]{2,1,0:T(8,128)(2,1)S(1)} %core_sum.9), channel_id=1, source_target_pairs={{0,2},{1,3},{2,0},{3,1},{4,6},{5,7},{6,4},{7,5},{8,10},{9,11},{10,... | collective-permute-start | bytes 1572872 | tf_op jit(solution)/shard_map/ppermute | solution.py:1112
  180.9 7.4 %collective-permute-start.45 = (bf16[4,64,512]{2,1,0:T(8,128)(2,1)S(1)}, bf16[4,64,512]{2,1,0:T(8,128)(2,1)S(1)}, u32[]{:S(2)}, u32[]{:S(2)}) collective-permute-start(bf16[4,64,512]{2,1,0:T(8,128)(2,1)S(1)} %get-tuple-element.295), channel_id=1, source_target_pairs={{0,4},{4,0},{8,12},{12,8},{16,20},{20,16},{24,28},{28,24},{1,5},{5... | collective-permute-start | bytes 786440 | tf_op jit(solution)/shard_map/ppermute | solution.py:1112
  182.4 11.5 %collective-permute-start.47 = (bf16[2,128,512]{2,1,0:T(8,128)(2,1)S(1)}, bf16[2,128,512]{2,1,0:T(8,128)(2,1)S(1)}, u32[]{:S(2)}, u32[]{:S(2)}) collective-permute-start(bf16[2,128,512]{2,1,0:T(8,128)(2,1)S(1)} %add.33.stay_ref), channel_id=1, source_target_pairs={{0,16},{4,20},{8,24},{12,28},{16,0},{20,4},{24,8},{28,12},{1,17},{... | collective-permute-start | bytes 786440 | tf_op jit(solution)/shard_map/ppermute | solution.py:1112
  186.0 5.7 %collective-permute-start.46 = (bf16[2,64,512]{2,1,0:T(8,128)(2,1)S(1)}, bf16[2,64,512]{2,1,0:T(8,128)(2,1)S(1)}, u32[]{:S(2)}, u32[]{:S(2)}) collective-permute-start(bf16[2,64,512]{2,1,0:T(8,128)(2,1)S(1)} %get-tuple-element.299), channel_id=1, source_target_pairs={{0,8},{4,12},{8,0},{12,4},{16,24},{20,28},{24,16},{28,20},{1,9},{5... | collective-permute-start | bytes 393224 | tf_op jit(solution)/shard_map/ppermute | solution.py:1112
  188.4 9.9 %collective-permute-start.50 = (bf16[4,72,512]{2,1,0:T(8,128)(2,1)S(1)}, bf16[4,72,512]{2,1,0:T(8,128)(2,1)S(1)}, u32[]{:S(2)}, u32[]{:S(2)}) collective-permute-start(bf16[4,72,512]{2,1,0:T(8,128)(2,1)S(1)} %get-tuple-element.305), channel_id=1, source_target_pairs={{0,4},{4,0},{8,12},{12,8},{16,20},{20,16},{24,28},{28,24},{1,5},{5... | collective-permute-start | bytes 884744 | tf_op jit(solution)/shard_map/ppermute | solution.py:1112
  194.0 15.1 %collective-permute-start.52 = (bf16[2,128,512]{2,1,0:T(8,128)(2,1)S(1)}, bf16[2,128,512]{2,1,0:T(8,128)(2,1)S(1)}, u32[]{:S(2)}, u32[]{:S(2)}) collective-permute-start(bf16[2,128,512]{2,1,0:T(8,128)(2,1)S(1)} %add.35.own_ref), channel_id=1, source_target_pairs={{0,8},{4,12},{8,0},{12,4},{16,24},{20,28},{24,16},{28,20},{1,9},{5... | collective-permute-start | bytes 786440 | tf_op jit(solution)/shard_map/ppermute | solution.py:1112
  194.8 11.3 %collective-permute-start.51 = (bf16[2,64,512]{2,1,0:T(8,128)(2,1)S(1)}, bf16[2,64,512]{2,1,0:T(8,128)(2,1)S(1)}, u32[]{:S(2)}, u32[]{:S(2)}) collective-permute-start(bf16[2,64,512]{2,1,0:T(8,128)(2,1)S(1)} %get-tuple-element.310), channel_id=1, source_target_pairs={{0,8},{4,12},{8,0},{12,4},{16,24},{20,28},{24,16},{28,20},{1,9},{5... | collective-permute-start | bytes 393224 | tf_op jit(solution)/shard_map/ppermute | solution.py:1112
  196.9 20.7 %collective-permute-start.55 = (bf16[4,64,512]{2,1,0:T(8,128)(2,1)S(1)}, bf16[4,64,512]{2,1,0:T(8,128)(2,1)S(1)}, u32[]{:S(2)}, u32[]{:S(2)}) collective-permute-start(bf16[4,64,512]{2,1,0:T(8,128)(2,1)S(1)} %get-tuple-element.317), channel_id=1, source_target_pairs={{0,4},{4,0},{8,12},{12,8},{16,20},{20,16},{24,28},{28,24},{1,5},{5... | collective-permute-start | bytes 786440 | tf_op jit(solution)/shard_map/ppermute | solution.py:1112
  198.9 12.0 %collective-permute-start.53 = (bf16[2,72,512]{2,1,0:T(8,128)(2,1)S(1)}, bf16[2,72,512]{2,1,0:T(8,128)(2,1)S(1)}, u32[]{:S(2)}, u32[]{:S(2)}) collective-permute-start(bf16[2,72,512]{2,1,0:T(8,128)(2,1)S(1)} %get-tuple-element.320), channel_id=1, source_target_pairs={{0,8},{4,12},{8,0},{12,4},{16,24},{20,28},{24,16},{28,20},{1,9},{5... | collective-permute-start | bytes 442376 | tf_op jit(solution)/shard_map/ppermute | solution.py:1112
  206.1 11.3 %collective-permute-start.54 = (bf16[2,64,512]{2,1,0:T(8,128)(2,1)S(1)}, bf16[2,64,512]{2,1,0:T(8,128)(2,1)S(1)}, u32[]{:S(2)}, u32[]{:S(2)}) collective-permute-start(bf16[2,64,512]{2,1,0:T(8,128)(2,1)S(1)} %add.36.stay_ref), channel_id=1, source_target_pairs={{0,16},{4,20},{8,24},{12,28},{16,0},{20,4},{24,8},{28,12},{1,17},{... | collective-permute-start | bytes 393224 | tf_op jit(solution)/shard_map/ppermute | solution.py:1112
  209.7 24.2 %collective-permute-start.61 = (bf16[4,128,512]{2,1,0:T(8,128)(2,1)S(1)}, bf16[4,128,512]{2,1,0:T(8,128)(2,1)S(1)}, u32[]{:S(2)}, u32[]{:S(2)}) collective-permute-start(bf16[4,128,512]{2,1,0:T(8,128)(2,1)S(1)} %join.5.refs_1_), channel_id=1, source_target_pairs={{0,4},{4,0},{8,12},{12,8},{16,20},{20,16},{24,28},{28,24},{1,5},{5... | collective-permute-start | bytes 1572872 | tf_op jit(solution)/shard_map/ppermute | solution.py:1112
  210.3 10.0 %collective-permute-start.56 = (bf16[2,64,512]{2,1,0:T(8,128)(2,1)S(1)}, bf16[2,64,512]{2,1,0:T(8,128)(2,1)S(1)}, u32[]{:S(2)}, u32[]{:S(2)}) collective-permute-start(bf16[2,64,512]{2,1,0:T(8,128)(2,1)S(1)} %add.34.stay_ref), channel_id=1, source_target_pairs={{0,16},{4,20},{8,24},{12,28},{16,0},{20,4},{24,8},{28,12},{1,17},{... | collective-permute-start | bytes 393224 | tf_op jit(solution)/shard_map/ppermute | solution.py:1112
  211.0 16.0 %collective-permute-start.58 = (bf16[2,72,512]{2,1,0:T(8,128)(2,1)S(1)}, bf16[2,72,512]{2,1,0:T(8,128)(2,1)S(1)}, u32[]{:S(2)}, u32[]{:S(2)}) collective-permute-start(bf16[2,72,512]{2,1,0:T(8,128)(2,1)S(1)} %add.37.stay_ref), channel_id=1, source_target_pairs={{0,16},{4,20},{8,24},{12,28},{16,0},{20,4},{24,8},{28,12},{1,17},{... | collective-permute-start | bytes 442376 | tf_op jit(solution)/shard_map/ppermute | solution.py:1112
  217.5 8.8 %collective-permute-start.57 = (bf16[2,64,512]{2,1,0:T(8,128)(2,1)S(1)}, bf16[2,64,512]{2,1,0:T(8,128)(2,1)S(1)}, u32[]{:S(2)}, u32[]{:S(2)}) collective-permute-start(bf16[2,64,512]{2,1,0:T(8,128)(2,1)S(1)} %add.38.own_ref), channel_id=1, source_target_pairs={{0,8},{4,12},{8,0},{12,4},{16,24},{20,28},{24,16},{28,20},{1,9},{5... | collective-permute-start | bytes 393224 | tf_op jit(solution)/shard_map/ppermute | solution.py:1112
  218.2 9.9 %collective-permute-start.59 = (bf16[2,64,512]{2,1,0:T(8,128)(2,1)S(1)}, bf16[2,64,512]{2,1,0:T(8,128)(2,1)S(1)}, u32[]{:S(2)}, u32[]{:S(2)}) collective-permute-start(bf16[2,64,512]{2,1,0:T(8,128)(2,1)S(1)} %get-tuple-element.329), channel_id=1, source_target_pairs={{0,8},{4,12},{8,0},{12,4},{16,24},{20,28},{24,16},{28,20},{1,9},{5... | collective-permute-start | bytes 393224 | tf_op jit(solution)/shard_map/ppermute | solution.py:1112
  220.3 9.2 %collective-permute-start.60 = (bf16[2,64,512]{2,1,0:T(8,128)(2,1)S(1)}, bf16[2,64,512]{2,1,0:T(8,128)(2,1)S(1)}, u32[]{:S(2)}, u32[]{:S(2)}) collective-permute-start(bf16[2,64,512]{2,1,0:T(8,128)(2,1)S(1)} %add.39.own_ref), channel_id=1, source_target_pairs={{0,8},{4,12},{8,0},{12,4},{16,24},{20,28},{24,16},{28,20},{1,9},{5... | collective-permute-start | bytes 393224 | tf_op jit(solution)/shard_map/ppermute | solution.py:1112
  226.9 7.0 %collective-permute-start.62 = (bf16[4,64,512]{2,1,0:T(8,128)(2,1)S(1)}, bf16[4,64,512]{2,1,0:T(8,128)(2,1)S(1)}, u32[]{:S(2)}, u32[]{:S(2)}) collective-permute-start(bf16[4,64,512]{2,1,0:T(8,128)(2,1)S(1)} %join.6.refs_3_), channel_id=1, source_target_pairs={{0,4},{4,0},{8,12},{12,8},{16,20},{20,16},{24,28},{28,24},{1,5},{5... | collective-permute-start | bytes 786440 | tf_op jit(solution)/shard_map/ppermute | solution.py:1112
  230.0 9.2 %collective-permute-start.64 = (bf16[4,64,512]{2,1,0:T(8,128)(2,1)S(1)}, bf16[4,64,512]{2,1,0:T(8,128)(2,1)S(1)}, u32[]{:S(2)}, u32[]{:S(2)}) collective-permute-start(bf16[4,64,512]{2,1,0:T(8,128)(2,1)S(1)} %join.7.refs_5_), channel_id=1, source_target_pairs={{0,4},{4,0},{8,12},{12,8},{16,20},{20,16},{24,28},{28,24},{1,5},{5... | collective-permute-start | bytes 786440 | tf_op jit(solution)/shard_map/ppermute | solution.py:1112
  230.7 6.4 %collective-permute-start.63 = (bf16[2,72,512]{2,1,0:T(8,128)(2,1)S(1)}, bf16[2,72,512]{2,1,0:T(8,128)(2,1)S(1)}, u32[]{:S(2)}, u32[]{:S(2)}) collective-permute-start(bf16[2,72,512]{2,1,0:T(8,128)(2,1)S(1)} %add.40.own_ref), channel_id=1, source_target_pairs={{0,8},{4,12},{8,0},{12,4},{16,24},{20,28},{24,16},{28,20},{1,9},{5... | collective-permute-start | bytes 442376 | tf_op jit(solution)/shard_map/ppermute | solution.py:1112
  230.7 8.6 %collective-permute-start.65 = (bf16[2,64,512]{2,1,0:T(8,128)(2,1)S(1)}, bf16[2,64,512]{2,1,0:T(8,128)(2,1)S(1)}, u32[]{:S(2)}, u32[]{:S(2)}) collective-permute-start(bf16[2,64,512]{2,1,0:T(8,128)(2,1)S(1)} %add.41.stay_ref), channel_id=1, source_target_pairs={{0,16},{4,20},{8,24},{12,28},{16,0},{20,4},{24,8},{28,12},{1,17},{... | collective-permute-start | bytes 393224 | tf_op jit(solution)/shard_map/ppermute | solution.py:1112
  239.3 5.0 %collective-permute-start.66 = (bf16[2,64,512]{2,1,0:T(8,128)(2,1)S(1)}, bf16[2,64,512]{2,1,0:T(8,128)(2,1)S(1)}, u32[]{:S(2)}, u32[]{:S(2)}) collective-permute-start(bf16[2,64,512]{2,1,0:T(8,128)(2,1)S(1)} %add.42.own_ref), channel_id=1, source_target_pairs={{0,8},{4,12},{8,0},{12,4},{16,24},{20,28},{24,16},{28,20},{1,9},{5... | collective-permute-start | bytes 393224 | tf_op jit(solution)/shard_map/ppermute | solution.py:1112
  239.4 10.6 %collective-permute-start.67 = (bf16[4,72,512]{2,1,0:T(8,128)(2,1)S(1)}, bf16[4,72,512]{2,1,0:T(8,128)(2,1)S(1)}, u32[]{:S(2)}, u32[]{:S(2)}) collective-permute-start(bf16[4,72,512]{2,1,0:T(8,128)(2,1)S(1)} %join.8.refs_1_), channel_id=1, source_target_pairs={{0,4},{4,0},{8,12},{12,8},{16,20},{20,16},{24,28},{28,24},{1,5},{5... | collective-permute-start | bytes 884744 | tf_op jit(solution)/shard_map/ppermute | solution.py:1112
  244.9 6.4 %collective-permute-start.68 = (bf16[4,64,512]{2,1,0:T(8,128)(2,1)S(1)}, bf16[4,64,512]{2,1,0:T(8,128)(2,1)S(1)}, u32[]{:S(2)}, u32[]{:S(2)}) collective-permute-start(bf16[4,64,512]{2,1,0:T(8,128)(2,1)S(1)} %join.9.refs_3_), channel_id=1, source_target_pairs={{0,4},{4,0},{8,12},{12,8},{16,20},{20,16},{24,28},{28,24},{1,5},{5... | collective-permute-start | bytes 786440 | tf_op jit(solution)/shard_map/ppermute | solution.py:1112
  (56 other events, 303.3 us)
